TPU v7x, 32 devices: a whole 2x2x4 slice. The times are simulated.
32 devices in a mesh: cfg: 2 (over x), seq: 8 (over z, y), dp: 2 (over core).
Axes of the slice: x: 2, y: 2, z: 4, core: 2. Of those that a mesh axis runs over, the one named last changes fastest.
Arguments:
- teacher_query: bfloat16 [2, 2, 2, 1024, 2048], P('cfg', None, 'dp', 'seq'), may hold values from -6 to 6
- teacher_key: bfloat16 [2, 2, 2, 1024, 2048], P('cfg', None, 'dp', 'seq'), may hold values from -6 to 6
- teacher_value: bfloat16 [2, 2, 2, 1024, 2048], P('cfg', None, 'dp', 'seq'), may hold values from -6 to 6
- hidden: bfloat16 [2, 2, 1024, 3072], P('cfg', 'dp', 'seq'), may hold values from -6 to 6
- adapter_down_weight: bfloat16 [3, 3072, 128], replicated, may hold values from -0.109375 to 0.109375
- adapter_up_weight: bfloat16 [3, 128, 2048], replicated, may hold values from -0.5 to 0.5
- guidance_index: int32 [2, 2], P(None, 'dp'), may hold values from 0 to 7
- timestep_index: int32 [2, 2], P(None, 'dp'), may hold values from 0 to 999
Outputs:
- student_out: bfloat16 [2, 2, 1024, 2048], P('cfg', 'dp', 'seq')
- grad_down: float32 [3, 3072, 128], P(None, ('cfg', 'seq', 'dp'))
- grad_up: float32 [3, 128, 2048], P(None, ('cfg', 'dp'), 'seq')
All inputs are finite; a program needn't handle non-finite values.
Results may differ from a plain program's by a relative error of at most 0.02.
The roundings to bfloat16 on the way count: a program that leaves them out, or rounds other values in their place, can miss the bound.
Values may be sent and summed in bfloat16 or wider, within the bound.
A program may use at most 128 MiB of HBM per device.

v0:
```python
import functools
import math

import jax
import jax.numpy as jnp
from jax import lax
from jax.experimental import pallas as pl
from jax.experimental.pallas import tpu as pltpu
from jax.sharding import PartitionSpec as P

HDIM = 128
ADAPTER_RANK = 128
TSTEPS = 1000
FACTOR = HDIM ** (-0.5)
FACTOR_BASE2 = FACTOR * math.log2(math.e)
VMEM_LIMIT = 60 * 1024 * 1024
BLOCK = 256
MESH = pl.DeviceIdType.MESH

NT = (((1,), (1,)), ((), ()))
TN = (((0,), (0,)), ((), ()))


def dot_f32(left, right):
    return jnp.dot(left, right, preferred_element_type=jnp.float32)


def dot_nt(left, right):
    return lax.dot_general(left, right, NT, preferred_element_type=jnp.float32)


def dot_tn(left, right):
    return lax.dot_general(left, right, TN, preferred_element_type=jnp.float32)


def inner_size(count):
    return max(size for size in range(1, count + 1) if count % size == 0 and size * size <= count)


def aligned(index, size):
    return pl.ds(pl.multiple_of(index * size, size), size)


def probs_by_key(key_head, query_block):
    scores = dot_nt(key_head, query_block)
    highest = jnp.max(scores, axis=0, keepdims=True)
    raised = jnp.exp2((scores - highest) * FACTOR_BASE2)
    return raised * (1.0 / jnp.sum(raised, axis=0, keepdims=True))


def step_kernel(
    sizes,
    out_scale,
    weight_ref,
    query_ref,
    key_ref,
    value_ref,
    hidden_ref,
    hidden_cols_ref,
    down_ref,
    up_ref,
    modulation_ref,
    tokens_ref,
    grad_down_ref,
    grad_up_ref,
    heads,
    hidden_own,
    hidden_all,
    down_own,
    up_own,
    ranks,
    weighted,
    weighted_in,
    target,
    s_query,
    s_key,
    s_value,
    key_t,
    value_t,
    grad_query,
    grad_key,
    grad_value,
    back_sum,
    back,
    back_in,
    student,
    up_parts,
    up_in,
    low,
    low_all,
    down_out,
    down_in,
    field_send,
    field_recv,
    pass_send,
    pass_recv,
    rank_send,
    rank_recv,
    fan_send,
    fan_recv,
    swap_send,
    swap_recv,
    out_send,
    out_recv,
    cols_send,
    cols_recv,
    up_send,
    up_recv,
    back_send,
    back_recv,
    low_send,
    low_recv,
    down_send,
    down_recv,
    local_sem,
):
    count, inner, dp_count = sizes
    outer = count // inner
    groups = 2 * inner * dp_count
    up_groups = 2 * dp_count
    fields = (query_ref, key_ref, value_ref)
    tok_here = query_ref.shape[1]
    length = tok_here * count
    columns = student.shape[1]
    heads_here = columns // HDIM
    step_rows = min(BLOCK, length)
    blocks = length // step_rows

    me = lax.axis_index("seq")
    cfg = lax.axis_index("cfg")
    dp = lax.axis_index("dp")
    other = 1 - cfg
    far = me // inner
    near = lax.rem(me, inner)
    group = (cfg * inner + near) * dp_count + dp
    up_group = cfg * dp_count + dp
    own_rows = aligned(me, tok_here)
    order = (other, cfg)

    def head_columns(head):
        return slice(head * HDIM, (head + 1) * HDIM)

    def seq_peer(step):
        return lax.rem(me + step, count)

    def group_device(step):
        peer = lax.rem(group + step, groups)
        rest = peer // dp_count
        return {
            "cfg": rest // inner,
            "seq": far * inner + lax.rem(rest, inner),
            "dp": lax.rem(peer, dp_count),
        }

    def remote(src, dst, send, recv, device):
        return pltpu.make_async_remote_copy(
            src_ref=src,
            dst_ref=dst,
            send_sem=send,
            recv_sem=recv,
            device_id=device,
            device_id_type=MESH,
        )

    loads = [
        pltpu.make_async_copy(hidden_ref, hidden_own, local_sem.at[0]),
        pltpu.make_async_copy(down_ref, down_own, local_sem.at[1]),
        pltpu.make_async_copy(
            up_ref.at[:, :, aligned(me, columns)], up_own, local_sem.at[2]
        ),
        pltpu.make_async_copy(hidden_cols_ref.at[group], hidden_all.at[group], local_sem.at[3]),
    ] + [
        pltpu.make_async_copy(
            fields[member].at[:, :, aligned(me, columns)],
            heads.at[member, 0:2, own_rows, :],
            local_sem.at[4 + member],
        )
        for member in range(3)
    ]
    for load in loads:
        load.start()

    barrier = pltpu.get_barrier_semaphore()
    for step in range(1, count):
        pl.semaphore_signal(
            barrier, inc=1, device_id={"seq": seq_peer(step)}, device_id_type=MESH
        )
    for step in range(1, groups):
        pl.semaphore_signal(barrier, inc=1, device_id=group_device(step), device_id_type=MESH)
    pl.semaphore_wait(barrier, count + groups - 2)

    def field_copy(phase, head, member, step):
        peer = seq_peer(step)
        half = order[phase]
        start = pl.multiple_of(peer * columns, columns) + head * HDIM
        return remote(
            fields[member].at[half, :, pl.ds(start, HDIM)],
            heads.at[member, half, own_rows, head_columns(head)],
            field_send.at[phase, head, member, step],
            field_recv.at[phase, head, member, step],
            {"seq": peer},
        )

    def start_fields(phase, head):
        for member in (1, 2, 0):
            for step in range(1, count):
                field_copy(phase, head, member, step).start()

    def wait_fields(phase, head):
        for member in (1, 2, 0):
            for step in range(1, count):
                field_copy(phase, head, member, step).wait_recv()

    def pass_copy(head, member):
        return remote(
            heads.at[member, 1, :, head_columns(head)],
            heads.at[member, 2, :, head_columns(head)],
            pass_send.at[head, member],
            pass_recv.at[head, member],
            {"cfg": other},
        )

    def rank_copy(step):
        return remote(
            ranks.at[far, near],
            ranks.at[far, near],
            rank_send.at[step],
            rank_recv.at[step],
            {"seq": lax.rem(far + step, outer) * inner + near},
        )

    def fan_copy(step):
        return remote(
            ranks.at[:, near],
            ranks.at[:, near],
            fan_send.at[step],
            fan_recv.at[step],
            {"seq": far * inner + lax.rem(near + step, inner)},
        )

    def swap_copy(head):
        return remote(
            weighted.at[head],
            weighted_in.at[head],
            swap_send.at[head],
            swap_recv.at[head],
            {"cfg": other},
        )

    def out_copy(head, step):
        peer = seq_peer(step)
        start = pl.multiple_of(me * columns, columns) + head * HDIM
        return remote(
            student.at[aligned(peer, tok_here), head_columns(head)],
            tokens_ref.at[:, pl.ds(start, HDIM)],
            out_send.at[head, step],
            out_recv.at[head, step],
            {"seq": peer},
        )

    def cols_copy(step):
        return remote(
            hidden_cols_ref.at[lax.rem(group + step, groups)],
            hidden_all.at[group],
            cols_send.at[step],
            cols_recv.at[step],
            group_device(step),
        )

    def up_copy(step):
        peer = lax.rem(up_group + step, up_groups)
        return remote(
            up_parts.at[peer],
            up_in.at[step],
            up_send.at[step],
            up_recv.at[step],
            {"cfg": peer // dp_count, "dp": lax.rem(peer, dp_count)},
        )

    def back_copy(step):
        peer = seq_peer(step)
        return remote(
            back.at[aligned(peer, tok_here), :],
            back_in.at[step],
            back_send.at[step],
            back_recv.at[step],
            {"seq": peer},
        )

    def low_copy(step):
        return remote(
            low, low_all.at[group], low_send.at[step], low_recv.at[step], group_device(step)
        )

    def down_copy(step):
        peer = lax.rem(far + step, outer)
        return remote(
            down_out.at[peer],
            down_in.at[step],
            down_send.at[step],
            down_recv.at[step],
            {"seq": peer * inner + near},
        )

    phases = [(phase, head) for phase in range(2) for head in range(heads_here)]
    start_fields(*phases[0])

    loads[0].wait()
    loads[1].wait()
    for member in range(3):
        projected = dot_f32(hidden_own[...], down_own[member]) * modulation_ref[...]
        ranks[far, near, :, head_columns(member)] = projected.astype(jnp.bfloat16)
    for step in range(1, outer):
        rank_copy(step).start()
    start_fields(*phases[1])
    for step in range(1, outer):
        rank_copy(step).wait_recv()
    for step in range(1, inner):
        fan_copy(step).start()
    for step in range(1, groups):
        cols_copy(step).start()
    for phase, head in phases[2:]:
        start_fields(phase, head)
    for load in loads[2:]:
        load.wait()

    def teacher(half, head, store):
        lanes = head_columns(head)
        value_t[...] = heads[2, half, :, lanes].T

        def one_block(step, _):
            rows = aligned(step, step_rows)
            weights = probs_by_key(heads[1, half, :, lanes], heads[0, half, rows, lanes])
            attended = dot_f32(value_t[...], weights.astype(jnp.bfloat16)).T
            store(rows, attended.astype(jnp.bfloat16).astype(jnp.float32))
            return 0

        lax.fori_loop(0, blocks, one_block, 0)

    for head in range(heads_here):
        wait_fields(0, head)

        @pl.when(cfg == 0)
        def _():
            for member in range(3):
                pass_copy(head, member).start()

        def store_other(rows, attended):
            weighted[head, rows, :] = (weight_ref[1] * attended).astype(jnp.bfloat16)

        teacher(other, head, store_other)
        swap_copy(head).start()

    for step in range(1, inner):
        fan_copy(step).wait_recv()

    for head in range(heads_here):
        lanes = head_columns(head)
        wait_fields(1, head)

        def store_own(rows, attended):
            target[rows, :] = weight_ref[0] * attended

        teacher(cfg, head, store_own)

        @pl.when(cfg == 1)
        def _():
            for member in range(3):
                pass_copy(head, member).wait_recv()

        for member, projected in enumerate((s_query, s_key, s_value)):
            low_rank = ranks[:, :, :, head_columns(member)].reshape(length, ADAPTER_RANK)
            frozen = heads[member, 2 * cfg, :, lanes].astype(jnp.float32)
            projected[...] = (frozen + dot_f32(low_rank, up_own[member, :, lanes])).astype(
                jnp.bfloat16
            )
        key_t[...] = s_key[...].T
        value_t[...] = s_value[...].T
        grad_key[...] = jnp.zeros_like(grad_key)
        grad_value[...] = jnp.zeros_like(grad_value)
        swap_copy(head).wait_recv()

        def one_block(step, _):
            rows = aligned(step, step_rows)
            query_block = s_query[rows, :]
            probability = probs_by_key(s_key[...], query_block)
            weights = probability.astype(jnp.bfloat16)
            attended = dot_f32(value_t[...], weights).T.astype(jnp.bfloat16)
            student[rows, lanes] = attended
            aim = target[rows, :] + weighted_in[head, rows, :].astype(jnp.float32)
            upstream = ((attended.astype(jnp.float32) - aim) * out_scale).astype(jnp.bfloat16)
            grad_value[...] += dot_f32(weights, upstream)
            prob_grad = dot_nt(s_value[...], upstream)
            center = jnp.sum(probability * prob_grad, axis=0, keepdims=True)
            score_grad = (probability * (prob_grad - center)).astype(jnp.bfloat16)
            grad_key[...] += dot_f32(score_grad, query_block)
            grad_query[rows, :] = (dot_f32(key_t[...], score_grad).T * FACTOR).astype(
                jnp.bfloat16
            )
            return 0

        lax.fori_loop(0, blocks, one_block, 0)
        for step in range(1, count):
            out_copy(head, step).start()

        gradients = (
            grad_query[...],
            (grad_key[...] * FACTOR).astype(jnp.bfloat16),
            grad_value[...].astype(jnp.bfloat16),
        )
        for member, gradient in enumerate(gradients):
            part = dot_nt(gradient, up_own[member, :, lanes])
            if head > 0:
                part = part + back_sum[:, head_columns(member)]
            if head < heads_here - 1:
                back_sum[:, head_columns(member)] = part
            else:
                back[:, head_columns(member)] = part.astype(jnp.bfloat16)
        if head == heads_here - 1:
            for step in range(1, count):
                back_copy(step).start()
        for member, gradient in enumerate(gradients):
            low_rank = ranks[:, :, :, head_columns(member)].reshape(length, ADAPTER_RANK)
            part = dot_tn(low_rank, gradient).astype(jnp.bfloat16)
            up_parts[:, member, :, lanes] = part.reshape(up_groups, -1, HDIM)

    for step in range(1, up_groups):
        up_copy(step).start()
    own_store = pltpu.make_async_copy(
        student.at[own_rows, :], tokens_ref.at[:, aligned(me, columns)], local_sem.at[7]
    )
    own_store.start()

    total = back[own_rows, :].astype(jnp.float32)
    for step in range(1, count):
        back_copy(step).wait_recv()
        total = total + back_in[step].astype(jnp.float32)
    scale = jnp.concatenate([modulation_ref[...]] * 3, axis=1)
    low_grad = (total * scale).astype(jnp.bfloat16)
    low[...] = low_grad
    low_all[group] = low_grad
    for step in range(1, groups):
        low_copy(step).start()

    up_total = up_parts[up_group].astype(jnp.float32)
    for step in range(1, up_groups):
        up_copy(step).wait_recv()
        up_total = up_total + up_in[step].astype(jnp.float32)
    grad_up_ref[...] = up_total

    for step in range(1, groups):
        cols_copy(step).wait_recv()
        low_copy(step).wait_recv()
    gathered_cols = hidden_all[...].reshape(groups * tok_here, -1)
    gathered_low = low_all[...].reshape(groups * tok_here, -1)
    down_rows = gathered_cols.shape[1] // outer
    partial = dot_tn(gathered_cols, gathered_low).astype(jnp.bfloat16)
    for peer in range(outer):
        down_out[peer] = partial[peer * down_rows : (peer + 1) * down_rows, :]
    for step in range(1, outer):
        down_copy(step).start()
    down_total = down_out[far].astype(jnp.float32)
    for step in range(1, outer):
        down_copy(step).wait_recv()
        down_total = down_total + down_in[step].astype(jnp.float32)
    for member in range(3):
        grad_down_ref[member] = down_total[:, head_columns(member)]

    own_store.wait()
    for phase, head in phases:
        for member in range(3):
            for step in range(1, count):
                field_copy(phase, head, member, step).wait_send()
    for head in range(heads_here):
        swap_copy(head).wait_send()

        @pl.when(cfg == 0)
        def _():
            for member in range(3):
                pass_copy(head, member).wait_send()

        for step in range(1, count):
            out_copy(head, step).wait()
    for step in range(1, outer):
        rank_copy(step).wait_send()
        down_copy(step).wait_send()
    for step in range(1, inner):
        fan_copy(step).wait_send()
    for step in range(1, groups):
        cols_copy(step).wait_send()
        low_copy(step).wait_send()
    for step in range(1, up_groups):
        up_copy(step).wait_send()
    for step in range(1, count):
        back_copy(step).wait_send()


def run_step(sizes, weights, fields, hidden, hidden_cols, down, up, modulation):
    count, inner, dp_count = sizes
    outer = count // inner
    groups, tok_here, group_cols = hidden_cols.shape
    up_groups = 2 * dp_count
    width = fields[0].shape[2]
    model_width = hidden.shape[1]
    length, columns = tok_here * count, width // count
    heads_here = columns // HDIM
    rank_cols = 3 * ADAPTER_RANK
    down_rows = group_cols // outer
    up_rows = ADAPTER_RANK // up_groups
    any_spec = pl.BlockSpec(memory_space=pl.ANY)
    vmem_spec = pl.BlockSpec(memory_space=pltpu.VMEM)

    def bf16(*shape):
        return pltpu.VMEM(shape, jnp.bfloat16)

    def f32(*shape):
        return pltpu.VMEM(shape, jnp.float32)

    def sems(*shape):
        return [pltpu.SemaphoreType.DMA(shape)] * 2

    total_rows = 2 * dp_count * length
    return pl.pallas_call(
        functools.partial(step_kernel, sizes, 1.0 / math.sqrt(total_rows)),
        out_shape=(
            jax.ShapeDtypeStruct((tok_here, width), jnp.bfloat16),
            jax.ShapeDtypeStruct((3, down_rows, ADAPTER_RANK), jnp.float32),
            jax.ShapeDtypeStruct((3, up_rows, columns), jnp.float32),
        ),
        in_specs=[pl.BlockSpec(memory_space=pltpu.SMEM)] + [any_spec] * 7 + [vmem_spec],
        out_specs=(any_spec, vmem_spec, vmem_spec),
        scratch_shapes=[
            bf16(3, 3, length, columns),
            bf16(tok_here, model_width),
            bf16(groups, tok_here, group_cols),
            bf16(3, model_width, ADAPTER_RANK),
            bf16(3, ADAPTER_RANK, columns),
            bf16(outer, inner, tok_here, rank_cols),
            bf16(heads_here, length, HDIM),
            bf16(heads_here, length, HDIM),
            f32(length, HDIM),
            bf16(length, HDIM),
            bf16(length, HDIM),
            bf16(length, HDIM),
            bf16(HDIM, length),
            bf16(HDIM, length),
            bf16(length, HDIM),
            f32(length, HDIM),
            f32(length, HDIM),
            f32(length, rank_cols),
            bf16(length, rank_cols),
            bf16(count, tok_here, rank_cols),
            bf16(length, columns),
            bf16(up_groups, 3, up_rows, columns),
            bf16(up_groups, 3, up_rows, columns),
            bf16(tok_here, rank_cols),
            bf16(groups, tok_here, rank_cols),
            bf16(outer, down_rows, rank_cols),
            bf16(outer, down_rows, rank_cols),
            *sems(2, heads_here, 3, count),
            *sems(heads_here, 3),
            *sems(outer),
            *sems(inner),
            *sems(heads_here),
            *sems(heads_here, count),
            *sems(groups),
            *sems(up_groups),
            *sems(count),
            *sems(groups),
            *sems(outer),
            pltpu.SemaphoreType.DMA((8,)),
        ],
        compiler_params=pltpu.CompilerParams(
            collective_id=0, has_side_effects=True, vmem_limit_bytes=VMEM_LIMIT
        ),
        name="step",
    )(weights, *fields, hidden, hidden_cols, down, up, modulation)


def body(
    teacher_query,
    teacher_key,
    teacher_value,
    hidden,
    adapter_down_weight,
    adapter_up_weight,
    guidance_index,
    timestep_index,
):
    cfg_index = lax.axis_index("cfg")
    seq_count = lax.axis_size("seq")
    dp_count = lax.axis_size("dp")
    inner = inner_size(seq_count)
    outer = seq_count // inner
    tok_here, model_width = hidden.shape[2:]
    groups = 2 * inner * dp_count

    guide_scale = 1.0 + 0.5 * guidance_index[:, 0].astype(jnp.float32)
    time_frac = (timestep_index[:, 0].astype(jnp.float32) + 0.5) / TSTEPS
    own_scale = lax.dynamic_index_in_dim(guide_scale, cfg_index, 0, keepdims=False)
    own_time = lax.dynamic_index_in_dim(time_frac, cfg_index, 0, keepdims=False)
    weighting = jnp.where(cfg_index == 0, guide_scale, 1.0 - guide_scale)
    weights = jnp.where(cfg_index == 0, weighting, weighting[::-1])
    rank_index = jnp.arange(1, ADAPTER_RANK + 1).astype(jnp.float32)
    modulation = 1.0 + 0.5 * jnp.cos(
        math.pi * rank_index * own_time + 0.25 * rank_index * own_scale
    )

    own_hidden = hidden[0, 0]
    hidden_cols = own_hidden.reshape(tok_here, 2, outer, inner, dp_count, -1)
    hidden_cols = hidden_cols.transpose(1, 3, 4, 0, 2, 5).reshape(groups, tok_here, -1)
    student_tokens, grad_down, grad_up = run_step(
        (seq_count, inner, dp_count),
        weights,
        (teacher_query[0, :, 0], teacher_key[0, :, 0], teacher_value[0, :, 0]),
        own_hidden,
        hidden_cols,
        adapter_down_weight,
        adapter_up_weight,
        modulation[None],
    )
    return (student_tokens[None, None], grad_down, grad_up)


def solution(mesh):
    placed = (
        P("cfg", None, "dp", "seq", None),
        P("cfg", None, "dp", "seq", None),
        P("cfg", None, "dp", "seq", None),
        P("cfg", "dp", "seq", None),
        P(),
        P(),
        P(None, "dp"),
        P(None, "dp"),
    )
    return jax.shard_map(
        body,
        mesh=mesh,
        in_specs=placed,
        out_specs=(
            P("cfg", "dp", "seq", None),
            P(None, ("cfg", "seq", "dp"), None),
            P(None, ("cfg", "dp"), "seq"),
        ),
        check_vma=False,
    )
```

profile of v0, /device:TPU:13, one launch (start us, length us, event | category | flops | bytes accessed | tf_op | source)
XLA Modules:
  0.0 159.3 jit_solution(7026468558126476407)
XLA Ops:
  0.6 0.7 add_multiply_fusion
  1.3 0.7 broadcast_select_fusion.1
  2.0 0.1 rev.3
  2.1 1.2 broadcast_select_fusion.weight_ref
  3.2 0.7 multiply_add_fusion
  3.9 0.6 fusion.2
  5.8 0.6 fusion.1.modulation_ref
  6.3 1.5 copy.12
  7.8 0.1 copy.13
  7.9 1.2 copy.14.hidden_cols_ref
  9.1 145.2 %step.1 = (bf16[128,2048]{1,0:T(8,128)(2,1)}, f32[3,96,128]{2,1,0:T(8,128)}, f32[3,32,256]{2,1,0:T(8,128)}) custom-call(f32[2]{0:T(128)} %broadcast_select_fusion.weight_ref, bf16[2,128,2048]{2,1,0:T(8,128)(2,1)} %bitcast.17, bf16[2,128,2048]{2,1,0:T(8,128)(2,1)} %bitcast.18, bf16[2,128,2048]{2,1,0:T(8,128)(2,1)} %bitcast.19, bf16[128,3072]{1,0:T(8,128)(2,1)} %bitcast.14, ...), custom_call_target="tpu_custom_call" | custom-call | tf_op jit(solution)/shard_map/step/pallas_call | solution.py:523
  154.3 1.9 %copy.18 = bf16[1,1,128,2048]{3,2,1,0:T(8,128)(2,1)} copy(bf16[1,1,128,2048]{3,2,1,0:T(8,128)(2,1)} %bitcast.20) | data formatting | bytes 1048576
  156.2 1.6 copy.19
  157.8 1.5 copy.20
where the time goes:
time: 160 us; the launch traced here: 159 us
  Pallas kernels  145 us (91%)
  local copies, waits for them, and re-layouts  7.83 us (5%)
  other arithmetic  4.3 us (3%)
  between operations  1.96 us (1%)
    pallas_call x1, Pallas kernels, run_step(): pl.pallas_call(functools.partial(step_kernel, sizes, 1.0 / math.sqrt(tota...  145 us
    unnamed x4, local copies, waits for them, and re-layouts  6.5 us

commit v1 on v0

--- a/solution.py
+++ b/solution.py
@@ -14,7 +14,7 @@
 FACTOR = HDIM ** (-0.5)
 FACTOR_BASE2 = FACTOR * math.log2(math.e)
 VMEM_LIMIT = 60 * 1024 * 1024
-BLOCK = 256
+BLOCK = 512
 MESH = pl.DeviceIdType.MESH
 
 NT = (((1,), (1,)), ((), ()))
@@ -51,20 +51,20 @@
 def step_kernel(
     sizes,
     out_scale,
-    weight_ref,
+    guide_ref,
+    time_ref,
     query_ref,
     key_ref,
     value_ref,
     hidden_ref,
-    hidden_cols_ref,
     down_ref,
     up_ref,
-    modulation_ref,
     tokens_ref,
     grad_down_ref,
     grad_up_ref,
     heads,
     hidden_own,
+    hidden_cols,
     hidden_all,
     down_own,
     up_own,
@@ -82,7 +82,9 @@
     grad_value,
     back_sum,
     back,
-    back_in,
+    near_in,
+    far_out,
+    far_in,
     student,
     up_parts,
     up_in,
@@ -106,17 +108,22 @@
     cols_recv,
     up_send,
     up_recv,
-    back_send,
-    back_recv,
+    near_send,
+    near_recv,
+    far_send,
+    far_recv,
     low_send,
     low_recv,
+    share_send,
+    share_recv,
     down_send,
     down_recv,
     local_sem,
 ):
     count, inner, dp_count = sizes
     outer = count // inner
-    groups = 2 * inner * dp_count
+    pairs = 2 * inner
+    groups = pairs * dp_count
     up_groups = 2 * dp_count
     fields = (query_ref, key_ref, value_ref)
     tok_here = query_ref.shape[1]
@@ -132,7 +139,8 @@
     other = 1 - cfg
     far = me // inner
     near = lax.rem(me, inner)
-    group = (cfg * inner + near) * dp_count + dp
+    pair = cfg * inner + near
+    group = dp * pairs + pair
     up_group = cfg * dp_count + dp
     own_rows = aligned(me, tok_here)
     order = (other, cfg)
@@ -143,14 +151,12 @@
     def seq_peer(step):
         return lax.rem(me + step, count)
 
+    def device_of(pair_index):
+        return {"cfg": pair_index // inner, "seq": far * inner + lax.rem(pair_index, inner)}
+
     def group_device(step):
         peer = lax.rem(group + step, groups)
-        rest = peer // dp_count
-        return {
-            "cfg": rest // inner,
-            "seq": far * inner + lax.rem(rest, inner),
-            "dp": lax.rem(peer, dp_count),
-        }
+        return {**device_of(lax.rem(peer, pairs)), "dp": peer // pairs}
 
     def remote(src, dst, send, recv, device):
         return pltpu.make_async_remote_copy(
@@ -168,12 +174,11 @@
         pltpu.make_async_copy(
             up_ref.at[:, :, aligned(me, columns)], up_own, local_sem.at[2]
         ),
-        pltpu.make_async_copy(hidden_cols_ref.at[group], hidden_all.at[group], local_sem.at[3]),
     ] + [
         pltpu.make_async_copy(
             fields[member].at[:, :, aligned(me, columns)],
             heads.at[member, 0:2, own_rows, :],
-            local_sem.at[4 + member],
+            local_sem.at[3 + member],
         )
         for member in range(3)
     ]
@@ -260,7 +265,7 @@
 
     def cols_copy(step):
         return remote(
-            hidden_cols_ref.at[lax.rem(group + step, groups)],
+            hidden_cols.at[lax.rem(group + step, groups)],
             hidden_all.at[group],
             cols_send.at[step],
             cols_recv.at[step],
@@ -277,19 +282,44 @@
             {"cfg": peer // dp_count, "dp": lax.rem(peer, dp_count)},
         )
 
-    def back_copy(step):
-        peer = seq_peer(step)
-        return remote(
-            back.at[aligned(peer, tok_here), :],
-            back_in.at[step],
-            back_send.at[step],
-            back_recv.at[step],
-            {"seq": peer},
+    def near_copy(far_step, step):
+        peer = lax.rem(near + step, inner)
+        row = lax.rem(far + far_step, outer)
+        return remote(
+            back.at[aligned(row * inner + peer, tok_here), :],
+            near_in.at[far_step, step],
+            near_send.at[far_step, step],
+            near_recv.at[far_step, step],
+            {"seq": far * inner + peer},
+        )
+
+    def far_copy(step):
+        return remote(
+            far_out.at[step],
+            far_in.at[step],
+            far_send.at[step],
+            far_recv.at[step],
+            {"seq": lax.rem(far + step, outer) * inner + near},
         )
 
     def low_copy(step):
         return remote(
-            low, low_all.at[group], low_send.at[step], low_recv.at[step], group_device(step)
+            low,
+            low_all.at[group],
+            low_send.at[step],
+            low_recv.at[step],
+            device_of(lax.rem(pair + step, pairs)),
+        )
+
+    def share_copy(pair_step, step):
+        source = lax.rem(pair - pair_step + pairs, pairs)
+        slot = low_all.at[dp * pairs + source]
+        return remote(
+            low if pair_step == 0 else slot,
+            slot,
+            share_send.at[pair_step, step],
+            share_recv.at[pair_step, step],
+            {"dp": lax.rem(dp + step, dp_count)},
         )
 
     def down_copy(step):
@@ -302,17 +332,40 @@
             {"seq": peer * inner + near},
         )
 
+    def guide_scale(half):
+        return 1.0 + 0.5 * guide_ref[half].astype(jnp.float32)
+
+    def weighting(half):
+        scale = guide_scale(half)
+        return jnp.where(cfg == 0, scale, 1.0 - scale)
+
+    rank_index = (lax.broadcasted_iota(jnp.int32, (1, ADAPTER_RANK), 1) + 1).astype(jnp.float32)
+    time_frac = (time_ref[cfg].astype(jnp.float32) + 0.5) / TSTEPS
+    modulation = 1.0 + 0.5 * jnp.cos(
+        math.pi * rank_index * time_frac + 0.25 * rank_index * guide_scale(cfg)
+    )
+
     phases = [(phase, head) for phase in range(2) for head in range(heads_here)]
     start_fields(*phases[0])
 
     loads[0].wait()
     loads[1].wait()
     for member in range(3):
-        projected = dot_f32(hidden_own[...], down_own[member]) * modulation_ref[...]
+        projected = dot_f32(hidden_own[...], down_own[member]) * modulation
         ranks[far, near, :, head_columns(member)] = projected.astype(jnp.bfloat16)
     for step in range(1, outer):
         rank_copy(step).start()
     start_fields(*phases[1])
+    rows_here = hidden_cols.shape[2] // outer
+    for block in range(outer * groups):
+        target_dp = block % dp_count
+        target_near = block // dp_count % inner
+        target_far = block // dp_count // inner % outer
+        target_pair = block // (dp_count * count) * inner + target_near
+        hidden_cols[
+            target_dp * pairs + target_pair, :, target_far * rows_here : (target_far + 1) * rows_here
+        ] = hidden_own[:, block * rows_here : (block + 1) * rows_here]
+    hidden_all[group] = hidden_cols[group]
     for step in range(1, outer):
         rank_copy(step).wait_recv()
     for step in range(1, inner):
@@ -324,18 +377,29 @@
     for load in loads[2:]:
         load.wait()
 
+    far_order = sorted(range(outer), key=lambda step: (step == 0, abs(2 * step - outer)))
+
+    def run_blocks(one_block):
+        unroll = 2 if blocks % 2 == 0 else 1
+
+        def some(step, _):
+            for offset in range(unroll):
+                one_block(step * unroll + offset)
+            return 0
+
+        lax.fori_loop(0, blocks // unroll, some, 0)
+
     def teacher(half, head, store):
         lanes = head_columns(head)
         value_t[...] = heads[2, half, :, lanes].T
 
-        def one_block(step, _):
+        def one_block(step):
             rows = aligned(step, step_rows)
             weights = probs_by_key(heads[1, half, :, lanes], heads[0, half, rows, lanes])
             attended = dot_f32(value_t[...], weights.astype(jnp.bfloat16)).T
             store(rows, attended.astype(jnp.bfloat16).astype(jnp.float32))
-            return 0
-
-        lax.fori_loop(0, blocks, one_block, 0)
+
+        run_blocks(one_block)
 
     for head in range(heads_here):
         wait_fields(0, head)
@@ -346,7 +410,7 @@
                 pass_copy(head, member).start()
 
         def store_other(rows, attended):
-            weighted[head, rows, :] = (weight_ref[1] * attended).astype(jnp.bfloat16)
+            weighted[head, rows, :] = (weighting(other) * attended).astype(jnp.bfloat16)
 
         teacher(other, head, store_other)
         swap_copy(head).start()
@@ -359,7 +423,7 @@
         wait_fields(1, head)
 
         def store_own(rows, attended):
-            target[rows, :] = weight_ref[0] * attended
+            target[rows, :] = weighting(cfg) * attended
 
         teacher(cfg, head, store_own)
 
@@ -380,7 +444,7 @@
         grad_value[...] = jnp.zeros_like(grad_value)
         swap_copy(head).wait_recv()
 
-        def one_block(step, _):
+        def one_block(step):
             rows = aligned(step, step_rows)
             query_block = s_query[rows, :]
             probability = probs_by_key(s_key[...], query_block)
@@ -397,11 +461,11 @@
             grad_query[rows, :] = (dot_f32(key_t[...], score_grad).T * FACTOR).astype(
                 jnp.bfloat16
             )
-            return 0
-
-        lax.fori_loop(0, blocks, one_block, 0)
-        for step in range(1, count):
-            out_copy(head, step).start()
+
+        run_blocks(one_block)
+        if head < heads_here - 1:
+            for step in range(1, count):
+                out_copy(head, step).start()
 
         gradients = (
             grad_query[...],
@@ -417,30 +481,49 @@
             else:
                 back[:, head_columns(member)] = part.astype(jnp.bfloat16)
         if head == heads_here - 1:
-            for step in range(1, count):
-                back_copy(step).start()
+            for far_step in far_order:
+                for step in range(1, inner):
+                    near_copy(far_step, step).start()
         for member, gradient in enumerate(gradients):
             low_rank = ranks[:, :, :, head_columns(member)].reshape(length, ADAPTER_RANK)
             part = dot_tn(low_rank, gradient).astype(jnp.bfloat16)
             up_parts[:, member, :, lanes] = part.reshape(up_groups, -1, HDIM)
 
+    for far_step in far_order:
+        row = lax.rem(far + far_step, outer)
+        part = back[aligned(row * inner + near, tok_here), :].astype(jnp.float32)
+        for step in range(1, inner):
+            near_copy(far_step, step).wait_recv()
+            part = part + near_in[far_step, step].astype(jnp.float32)
+        if far_step > 0:
+            far_out[far_step] = part.astype(jnp.bfloat16)
+            far_copy(far_step).start()
+        else:
+            total = part
+    for step in range(1, count):
+        out_copy(heads_here - 1, step).start()
     for step in range(1, up_groups):
         up_copy(step).start()
     own_store = pltpu.make_async_copy(
-        student.at[own_rows, :], tokens_ref.at[:, aligned(me, columns)], local_sem.at[7]
+        student.at[own_rows, :], tokens_ref.at[:, aligned(me, columns)], local_sem.at[6]
     )
     own_store.start()
 
-    total = back[own_rows, :].astype(jnp.float32)
-    for step in range(1, count):
-        back_copy(step).wait_recv()
-        total = total + back_in[step].astype(jnp.float32)
-    scale = jnp.concatenate([modulation_ref[...]] * 3, axis=1)
+    for step in range(1, outer):
+        far_copy(step).wait_recv()
+        total = total + far_in[step].astype(jnp.float32)
+    scale = jnp.concatenate([modulation] * 3, axis=1)
     low_grad = (total * scale).astype(jnp.bfloat16)
     low[...] = low_grad
     low_all[group] = low_grad
-    for step in range(1, groups):
+    for step in range(1, pairs):
         low_copy(step).start()
+    for step in range(1, dp_count):
+        share_copy(0, step).start()
+    for pair_step in range(1, pairs):
+        low_copy(pair_step).wait_recv()
+        for step in range(1, dp_count):
+            share_copy(pair_step, step).start()
 
     up_total = up_parts[up_group].astype(jnp.float32)
     for step in range(1, up_groups):
@@ -450,7 +533,9 @@
 
     for step in range(1, groups):
         cols_copy(step).wait_recv()
-        low_copy(step).wait_recv()
+    for pair_step in range(pairs):
+        for step in range(1, dp_count):
+            share_copy(pair_step, step).wait_recv()
     gathered_cols = hidden_all[...].reshape(groups * tok_here, -1)
     gathered_low = low_all[...].reshape(groups * tok_here, -1)
     down_rows = gathered_cols.shape[1] // outer
@@ -488,27 +573,37 @@
         fan_copy(step).wait_send()
     for step in range(1, groups):
         cols_copy(step).wait_send()
-        low_copy(step).wait_send()
+    for pair_step in range(pairs):
+        if pair_step > 0:
+            low_copy(pair_step).wait_send()
+        for step in range(1, dp_count):
+            share_copy(pair_step, step).wait_send()
     for step in range(1, up_groups):
         up_copy(step).wait_send()
-    for step in range(1, count):
-        back_copy(step).wait_send()
-
-
-def run_step(sizes, weights, fields, hidden, hidden_cols, down, up, modulation):
+    for far_step in range(outer):
+        if far_step > 0:
+            far_copy(far_step).wait_send()
+        for step in range(1, inner):
+            near_copy(far_step, step).wait_send()
+
+
+def run_step(sizes, guide, time_index, fields, hidden, down, up):
     count, inner, dp_count = sizes
     outer = count // inner
-    groups, tok_here, group_cols = hidden_cols.shape
+    pairs = 2 * inner
+    groups = pairs * dp_count
     up_groups = 2 * dp_count
-    width = fields[0].shape[2]
+    tok_here, width = fields[0].shape[1:]
     model_width = hidden.shape[1]
     length, columns = tok_here * count, width // count
     heads_here = columns // HDIM
     rank_cols = 3 * ADAPTER_RANK
+    group_cols = model_width // groups
     down_rows = group_cols // outer
     up_rows = ADAPTER_RANK // up_groups
     any_spec = pl.BlockSpec(memory_space=pl.ANY)
     vmem_spec = pl.BlockSpec(memory_space=pltpu.VMEM)
+    smem_spec = pl.BlockSpec(memory_space=pltpu.SMEM)
 
     def bf16(*shape):
         return pltpu.VMEM(shape, jnp.bfloat16)
@@ -527,11 +622,12 @@
             jax.ShapeDtypeStruct((3, down_rows, ADAPTER_RANK), jnp.float32),
             jax.ShapeDtypeStruct((3, up_rows, columns), jnp.float32),
         ),
-        in_specs=[pl.BlockSpec(memory_space=pltpu.SMEM)] + [any_spec] * 7 + [vmem_spec],
+        in_specs=[smem_spec] * 2 + [any_spec] * 6,
         out_specs=(any_spec, vmem_spec, vmem_spec),
         scratch_shapes=[
             bf16(3, 3, length, columns),
             bf16(tok_here, model_width),
+            bf16(groups, tok_here, group_cols),
             bf16(groups, tok_here, group_cols),
             bf16(3, model_width, ADAPTER_RANK),
             bf16(3, ADAPTER_RANK, columns),
@@ -549,7 +645,9 @@
             f32(length, HDIM),
             f32(length, rank_cols),
             bf16(length, rank_cols),
-            bf16(count, tok_here, rank_cols),
+            bf16(outer, inner, tok_here, rank_cols),
+            bf16(outer, tok_here, rank_cols),
+            bf16(outer, tok_here, rank_cols),
             bf16(length, columns),
             bf16(up_groups, 3, up_rows, columns),
             bf16(up_groups, 3, up_rows, columns),
@@ -565,16 +663,43 @@
             *sems(heads_here, count),
             *sems(groups),
             *sems(up_groups),
-            *sems(count),
-            *sems(groups),
+            *sems(outer, inner),
             *sems(outer),
-            pltpu.SemaphoreType.DMA((8,)),
+            *sems(pairs),
+            *sems(pairs, dp_count),
+            *sems(outer),
+            pltpu.SemaphoreType.DMA((7,)),
         ],
         compiler_params=pltpu.CompilerParams(
             collective_id=0, has_side_effects=True, vmem_limit_bytes=VMEM_LIMIT
         ),
         name="step",
-    )(weights, *fields, hidden, hidden_cols, down, up, modulation)
+    )(guide, time_index, *fields, hidden, down, up)
+
+
+def emit_kernel(*refs):
+    half = len(refs) // 2
+    sems = refs[-1]
+    copies = [
+        pltpu.make_async_copy(refs[item], refs[half + item], sems.at[item])
+        for item in range(half)
+    ]
+    for copy in copies:
+        copy.start()
+    for copy in copies:
+        copy.wait()
+
+
+def emit(arrays):
+    return pl.pallas_call(
+        emit_kernel,
+        out_shape=tuple(jax.ShapeDtypeStruct(array.shape, array.dtype) for array in arrays),
+        in_specs=[pl.BlockSpec(memory_space=pltpu.VMEM)] * len(arrays),
+        out_specs=(pl.BlockSpec(memory_space=pl.ANY),) * len(arrays),
+        scratch_shapes=[pltpu.SemaphoreType.DMA((len(arrays),))],
+        compiler_params=pltpu.CompilerParams(vmem_limit_bytes=4 * 1024 * 1024),
+        name="emit",
+    )(*arrays)
 
 
 def body(
@@ -587,38 +712,17 @@
     guidance_index,
     timestep_index,
 ):
-    cfg_index = lax.axis_index("cfg")
     seq_count = lax.axis_size("seq")
-    dp_count = lax.axis_size("dp")
-    inner = inner_size(seq_count)
-    outer = seq_count // inner
-    tok_here, model_width = hidden.shape[2:]
-    groups = 2 * inner * dp_count
-
-    guide_scale = 1.0 + 0.5 * guidance_index[:, 0].astype(jnp.float32)
-    time_frac = (timestep_index[:, 0].astype(jnp.float32) + 0.5) / TSTEPS
-    own_scale = lax.dynamic_index_in_dim(guide_scale, cfg_index, 0, keepdims=False)
-    own_time = lax.dynamic_index_in_dim(time_frac, cfg_index, 0, keepdims=False)
-    weighting = jnp.where(cfg_index == 0, guide_scale, 1.0 - guide_scale)
-    weights = jnp.where(cfg_index == 0, weighting, weighting[::-1])
-    rank_index = jnp.arange(1, ADAPTER_RANK + 1).astype(jnp.float32)
-    modulation = 1.0 + 0.5 * jnp.cos(
-        math.pi * rank_index * own_time + 0.25 * rank_index * own_scale
-    )
-
-    own_hidden = hidden[0, 0]
-    hidden_cols = own_hidden.reshape(tok_here, 2, outer, inner, dp_count, -1)
-    hidden_cols = hidden_cols.transpose(1, 3, 4, 0, 2, 5).reshape(groups, tok_here, -1)
-    student_tokens, grad_down, grad_up = run_step(
-        (seq_count, inner, dp_count),
-        weights,
+    outputs = run_step(
+        (seq_count, inner_size(seq_count), lax.axis_size("dp")),
+        guidance_index[:, 0],
+        timestep_index[:, 0],
         (teacher_query[0, :, 0], teacher_key[0, :, 0], teacher_value[0, :, 0]),
-        own_hidden,
-        hidden_cols,
+        hidden[0, 0],
         adapter_down_weight,
         adapter_up_weight,
-        modulation[None],
     )
+    student_tokens, grad_down, grad_up = emit(outputs)
     return (student_tokens[None, None], grad_down, grad_up)
 
 

time: 160 us -> 135 us (0.84)
  the two profiles are of different devices: /device:TPU:13 before, /device:TPU:0 now
where the time goes in v1:
time: 135 us; the launch traced here: 134 us
  Pallas kernels  130 us (96%)
  local copies, waits for them, and re-layouts  2.84 us (2%)
    pallas_call x1, Pallas kernels, run_step(): pl.pallas_call(functools.partial(step_kernel, sizes, 1.0 / math.sqrt(tota...  129 us
    unnamed x6, local copies, waits for them, and re-layouts  2.84 us

profile of v1, /device:TPU:0, one launch (start us, length us, event | category | flops | bytes accessed | tf_op | source)
XLA Modules:
  0.0 133.9 jit_solution(536495581691730781)
XLA Ops:
  0.6 129.4 %step.1 = (bf16[128,2048]{1,0:T(8,128)(2,1)}, f32[3,96,128]{2,1,0:T(8,128)}, f32[3,32,256]{2,1,0:T(8,128)}) custom-call(s32[2]{0:T(128)} %bitcast.11, s32[2]{0:T(128)} %bitcast.12, bf16[2,128,2048]{2,1,0:T(8,128)(2,1)} %bitcast.7, bf16[2,128,2048]{2,1,0:T(8,128)(2,1)} %bitcast.8, bf16[2,128,2048]{2,1,0:T(8,128)(2,1)} %bitcast.9, bf16[128,3072]{1,0:T(8,128)(2,1)} %bitcast.10, ...), custom_call_target="tpu_custom_call" | custom-call | tf_op jit(solution)/shard_map/step/pallas_call | solution.py:618
  130.0 0.0 copy-start
  130.0 1.0 copy-done
  131.1 0.0 copy-start.1
  131.1 0.9 copy-done.1
  132.0 0.0 copy-start.2
  132.0 0.9 copy-done.2
  132.9 0.9 emit.1
Async XLA Ops:
  130.0 1.0 copy-start
  131.1 0.9 copy-start.1
  132.0 0.9 copy-start.2

commit v2 on v1

--- a/solution.py
+++ b/solution.py
@@ -66,6 +66,7 @@
     hidden_own,
     hidden_cols,
     hidden_all,
+    hidden_t,
     down_own,
     up_own,
     ranks,
@@ -192,8 +193,6 @@
         )
     for step in range(1, groups):
         pl.semaphore_signal(barrier, inc=1, device_id=group_device(step), device_id_type=MESH)
-    pl.semaphore_wait(barrier, count + groups - 2)
-
     def field_copy(phase, head, member, step):
         peer = seq_peer(step)
         half = order[phase]
@@ -206,10 +205,9 @@
             {"seq": peer},
         )
 
-    def start_fields(phase, head):
-        for member in (1, 2, 0):
-            for step in range(1, count):
-                field_copy(phase, head, member, step).start()
+    def start_fields(phase, head, member):
+        for step in range(1, count):
+            field_copy(phase, head, member, step).start()
 
     def wait_fields(phase, head):
         for member in (1, 2, 0):
@@ -225,14 +223,31 @@
             {"cfg": other},
         )
 
-    def rank_copy(step):
-        return remote(
-            ranks.at[far, near],
-            ranks.at[far, near],
-            rank_send.at[step],
-            rank_recv.at[step],
-            {"seq": lax.rem(far + step, outer) * inner + near},
-        )
+    def rank_copy(way, hop):
+        toward, back_by = (1, outer - hop) if way == 0 else (outer - 1, hop)
+        block = ranks.at[lax.rem(far + back_by, outer), near]
+        return remote(
+            block,
+            block,
+            rank_send.at[way, hop],
+            rank_recv.at[way, hop],
+            {"seq": lax.rem(far + toward, outer) * inner + near},
+        )
+
+    def ranks_leave(way, hop):
+        if way == 0:
+            return jnp.logical_and(far >= hop, far < outer - 1)
+        return jnp.logical_and(far < outer - hop, far > 0)
+
+    def ranks_come(way, hop):
+        return far > hop if way == 0 else far < outer - 1 - hop
+
+    def rank_step(hop, action, test):
+        for way in range(2):
+
+            @pl.when(test(way, hop))
+            def _():
+                getattr(rank_copy(way, hop), action)()
 
     def fan_copy(step):
         return remote(
@@ -282,53 +297,54 @@
             {"cfg": peer // dp_count, "dp": lax.rem(peer, dp_count)},
         )
 
-    def near_copy(far_step, step):
+    def near_copy(member, far_step, step):
         peer = lax.rem(near + step, inner)
         row = lax.rem(far + far_step, outer)
         return remote(
-            back.at[aligned(row * inner + peer, tok_here), :],
-            near_in.at[far_step, step],
-            near_send.at[far_step, step],
-            near_recv.at[far_step, step],
+            back.at[aligned(row * inner + peer, tok_here), head_columns(member)],
+            near_in.at[far_step, step, :, head_columns(member)],
+            near_send.at[member, far_step, step],
+            near_recv.at[member, far_step, step],
             {"seq": far * inner + peer},
         )
 
-    def far_copy(step):
-        return remote(
-            far_out.at[step],
-            far_in.at[step],
-            far_send.at[step],
-            far_recv.at[step],
+    def far_copy(member, step):
+        return remote(
+            far_out.at[step, :, head_columns(member)],
+            far_in.at[step, :, head_columns(member)],
+            far_send.at[member, step],
+            far_recv.at[member, step],
             {"seq": lax.rem(far + step, outer) * inner + near},
         )
 
-    def low_copy(step):
-        return remote(
-            low,
-            low_all.at[group],
-            low_send.at[step],
-            low_recv.at[step],
+    def low_copy(member, step):
+        return remote(
+            low.at[:, head_columns(member)],
+            low_all.at[group, :, head_columns(member)],
+            low_send.at[member, step],
+            low_recv.at[member, step],
             device_of(lax.rem(pair + step, pairs)),
         )
 
-    def share_copy(pair_step, step):
+    def share_copy(member, pair_step, step):
         source = lax.rem(pair - pair_step + pairs, pairs)
-        slot = low_all.at[dp * pairs + source]
-        return remote(
-            low if pair_step == 0 else slot,
+        lanes = head_columns(member)
+        slot = low_all.at[dp * pairs + source, :, lanes]
+        return remote(
+            low.at[:, lanes] if pair_step == 0 else slot,
             slot,
-            share_send.at[pair_step, step],
-            share_recv.at[pair_step, step],
+            share_send.at[member, pair_step, step],
+            share_recv.at[member, pair_step, step],
             {"dp": lax.rem(dp + step, dp_count)},
         )
 
-    def down_copy(step):
+    def down_copy(member, step):
         peer = lax.rem(far + step, outer)
         return remote(
-            down_out.at[peer],
-            down_in.at[step],
-            down_send.at[step],
-            down_recv.at[step],
+            down_out.at[peer, :, head_columns(member)],
+            down_in.at[step, :, head_columns(member)],
+            down_send.at[member, step],
+            down_recv.at[member, step],
             {"seq": peer * inner + near},
         )
 
@@ -346,16 +362,28 @@
     )
 
     phases = [(phase, head) for phase in range(2) for head in range(heads_here)]
-    start_fields(*phases[0])
-
     loads[0].wait()
     loads[1].wait()
     for member in range(3):
         projected = dot_f32(hidden_own[...], down_own[member]) * modulation
         ranks[far, near, :, head_columns(member)] = projected.astype(jnp.bfloat16)
-    for step in range(1, outer):
-        rank_copy(step).start()
-    start_fields(*phases[1])
+    pl.semaphore_wait(barrier, count + groups - 2)
+
+    sends = [(phase, head, member) for phase, head in phases for member in (1, 2, 0)]
+    sent = 0
+    for hop in range(outer - 1):
+        if hop > 0:
+            rank_step(hop - 1, "wait_recv", ranks_come)
+        rank_step(hop, "start", ranks_leave)
+        start_fields(*sends[sent])
+        sent += 1
+    for turn in sends[sent : 2 * sent]:
+        start_fields(*turn)
+    rank_step(outer - 2, "wait_recv", ranks_come)
+    for step in range(1, inner):
+        fan_copy(step).start()
+    for turn in sends[2 * sent :]:
+        start_fields(*turn)
     rows_here = hidden_cols.shape[2] // outer
     for block in range(outer * groups):
         target_dp = block % dp_count
@@ -366,14 +394,8 @@
             target_dp * pairs + target_pair, :, target_far * rows_here : (target_far + 1) * rows_here
         ] = hidden_own[:, block * rows_here : (block + 1) * rows_here]
     hidden_all[group] = hidden_cols[group]
-    for step in range(1, outer):
-        rank_copy(step).wait_recv()
-    for step in range(1, inner):
-        fan_copy(step).start()
     for step in range(1, groups):
         cols_copy(step).start()
-    for phase, head in phases[2:]:
-        start_fields(phase, head)
     for load in loads[2:]:
         load.wait()
 
@@ -480,50 +502,83 @@
                 back_sum[:, head_columns(member)] = part
             else:
                 back[:, head_columns(member)] = part.astype(jnp.bfloat16)
+                for far_step in far_order:
+                    for step in range(1, inner):
+                        near_copy(member, far_step, step).start()
         if head == heads_here - 1:
-            for far_step in far_order:
-                for step in range(1, inner):
-                    near_copy(far_step, step).start()
+            for step in range(1, count):
+                out_copy(head, step).start()
         for member, gradient in enumerate(gradients):
             low_rank = ranks[:, :, :, head_columns(member)].reshape(length, ADAPTER_RANK)
             part = dot_tn(low_rank, gradient).astype(jnp.bfloat16)
             up_parts[:, member, :, lanes] = part.reshape(up_groups, -1, HDIM)
 
-    for far_step in far_order:
-        row = lax.rem(far + far_step, outer)
-        part = back[aligned(row * inner + near, tok_here), :].astype(jnp.float32)
-        for step in range(1, inner):
-            near_copy(far_step, step).wait_recv()
-            part = part + near_in[far_step, step].astype(jnp.float32)
-        if far_step > 0:
-            far_out[far_step] = part.astype(jnp.bfloat16)
-            far_copy(far_step).start()
-        else:
-            total = part
-    for step in range(1, count):
-        out_copy(heads_here - 1, step).start()
     for step in range(1, up_groups):
         up_copy(step).start()
     own_store = pltpu.make_async_copy(
         student.at[own_rows, :], tokens_ref.at[:, aligned(me, columns)], local_sem.at[6]
     )
     own_store.start()
-
-    for step in range(1, outer):
-        far_copy(step).wait_recv()
-        total = total + far_in[step].astype(jnp.float32)
-    scale = jnp.concatenate([modulation] * 3, axis=1)
-    low_grad = (total * scale).astype(jnp.bfloat16)
-    low[...] = low_grad
-    low_all[group] = low_grad
-    for step in range(1, pairs):
-        low_copy(step).start()
-    for step in range(1, dp_count):
-        share_copy(0, step).start()
-    for pair_step in range(1, pairs):
-        low_copy(pair_step).wait_recv()
+    for step in range(1, groups):
+        cols_copy(step).wait_recv()
+    gathered_cols = hidden_all[...].reshape(groups * tok_here, -1)
+    hidden_t[...] = gathered_cols.T
+    down_rows = gathered_cols.shape[1] // outer
+
+    def reduce_near(member):
+        lanes = head_columns(member)
+        for far_step in far_order:
+            row = lax.rem(far + far_step, outer)
+            part = back[aligned(row * inner + near, tok_here), lanes].astype(jnp.float32)
+            for step in range(1, inner):
+                near_copy(member, far_step, step).wait_recv()
+                part = part + near_in[far_step, step, :, lanes].astype(jnp.float32)
+            if far_step > 0:
+                far_out[far_step, :, lanes] = part.astype(jnp.bfloat16)
+                far_copy(member, far_step).start()
+        return part
+
+    def reduce_far(member, total):
+        lanes = head_columns(member)
+        for step in range(1, outer):
+            far_copy(member, step).wait_recv()
+            total = total + far_in[step, :, lanes].astype(jnp.float32)
+        low_grad = (total * modulation).astype(jnp.bfloat16)
+        low[:, lanes] = low_grad
+        low_all[group, :, lanes] = low_grad
+        for step in range(1, pairs):
+            low_copy(member, step).start()
         for step in range(1, dp_count):
-            share_copy(pair_step, step).start()
+            share_copy(member, 0, step).start()
+
+    def spread(member):
+        for pair_step in range(1, pairs):
+            low_copy(member, pair_step).wait_recv()
+            for step in range(1, dp_count):
+                share_copy(member, pair_step, step).start()
+
+    def contract(member):
+        lanes = head_columns(member)
+        for pair_step in range(pairs):
+            for step in range(1, dp_count):
+                share_copy(member, pair_step, step).wait_recv()
+        gathered_low = low_all[:, :, lanes].reshape(groups * tok_here, ADAPTER_RANK)
+        partial = dot_f32(hidden_t[...], gathered_low).astype(jnp.bfloat16)
+        for peer in range(outer):
+            down_out[peer, :, lanes] = partial[peer * down_rows : (peer + 1) * down_rows, :]
+        for step in range(1, outer):
+            down_copy(member, step).start()
+
+    totals = {}
+    for turn in range(6):
+        if turn < 3:
+            totals[turn] = reduce_near(turn)
+        if 1 <= turn < 4:
+            reduce_far(turn - 1, totals[turn - 1])
+        if 2 <= turn < 5:
+            spread(turn - 2)
+        if turn >= 3:
+            contract(turn - 3)
 
     up_total = up_parts[up_group].astype(jnp.float32)
     for step in range(1, up_groups):
@@ -531,25 +586,13 @@
         up_total = up_total + up_in[step].astype(jnp.float32)
     grad_up_ref[...] = up_total
 
-    for step in range(1, groups):
-        cols_copy(step).wait_recv()
-    for pair_step in range(pairs):
-        for step in range(1, dp_count):
-            share_copy(pair_step, step).wait_recv()
-    gathered_cols = hidden_all[...].reshape(groups * tok_here, -1)
-    gathered_low = low_all[...].reshape(groups * tok_here, -1)
-    down_rows = gathered_cols.shape[1] // outer
-    partial = dot_tn(gathered_cols, gathered_low).astype(jnp.bfloat16)
-    for peer in range(outer):
-        down_out[peer] = partial[peer * down_rows : (peer + 1) * down_rows, :]
-    for step in range(1, outer):
-        down_copy(step).start()
-    down_total = down_out[far].astype(jnp.float32)
-    for step in range(1, outer):
-        down_copy(step).wait_recv()
-        down_total = down_total + down_in[step].astype(jnp.float32)
     for member in range(3):
-        grad_down_ref[member] = down_total[:, head_columns(member)]
+        lanes = head_columns(member)
+        down_total = down_out[far, :, lanes].astype(jnp.float32)
+        for step in range(1, outer):
+            down_copy(member, step).wait_recv()
+            down_total = down_total + down_in[step, :, lanes].astype(jnp.float32)
+        grad_down_ref[member] = down_total
 
     own_store.wait()
     for phase, head in phases:
@@ -566,25 +609,26 @@
 
         for step in range(1, count):
             out_copy(head, step).wait()
-    for step in range(1, outer):
-        rank_copy(step).wait_send()
-        down_copy(step).wait_send()
+    for hop in range(outer - 1):
+        rank_step(hop, "wait_send", ranks_leave)
     for step in range(1, inner):
         fan_copy(step).wait_send()
     for step in range(1, groups):
         cols_copy(step).wait_send()
-    for pair_step in range(pairs):
-        if pair_step > 0:
-            low_copy(pair_step).wait_send()
-        for step in range(1, dp_count):
-            share_copy(pair_step, step).wait_send()
     for step in range(1, up_groups):
         up_copy(step).wait_send()
-    for far_step in range(outer):
-        if far_step > 0:
-            far_copy(far_step).wait_send()
-        for step in range(1, inner):
-            near_copy(far_step, step).wait_send()
+    for member in range(3):
+        for pair_step in range(pairs):
+            if pair_step > 0:
+                low_copy(member, pair_step).wait_send()
+            for step in range(1, dp_count):
+                share_copy(member, pair_step, step).wait_send()
+        for far_step in range(outer):
+            if far_step > 0:
+                far_copy(member, far_step).wait_send()
+                down_copy(member, far_step).wait_send()
+            for step in range(1, inner):
+                near_copy(member, far_step, step).wait_send()
 
 
 def run_step(sizes, guide, time_index, fields, hidden, down, up):
@@ -629,6 +673,7 @@
             bf16(tok_here, model_width),
             bf16(groups, tok_here, group_cols),
             bf16(groups, tok_here, group_cols),
+            bf16(group_cols, groups * tok_here),
             bf16(3, model_width, ADAPTER_RANK),
             bf16(3, ADAPTER_RANK, columns),
             bf16(outer, inner, tok_here, rank_cols),
@@ -657,17 +702,17 @@
             bf16(outer, down_rows, rank_cols),
             *sems(2, heads_here, 3, count),
             *sems(heads_here, 3),
-            *sems(outer),
+            *sems(2, outer),
             *sems(inner),
             *sems(heads_here),
             *sems(heads_here, count),
             *sems(groups),
             *sems(up_groups),
-            *sems(outer, inner),
-            *sems(outer),
-            *sems(pairs),
-            *sems(pairs, dp_count),
-            *sems(outer),
+            *sems(3, outer, inner),
+            *sems(3, outer),
+            *sems(3, pairs),
+            *sems(3, pairs, dp_count),
+            *sems(3, outer),
             pltpu.SemaphoreType.DMA((7,)),
         ],
         compiler_params=pltpu.CompilerParams(
@@ -678,26 +723,35 @@
 
 
 def emit_kernel(*refs):
-    half = len(refs) // 2
-    sems = refs[-1]
-    copies = [
-        pltpu.make_async_copy(refs[item], refs[half + item], sems.at[item])
-        for item in range(half)
+    count = (len(refs) - 2) // 3
+    held = refs[2 * count : 3 * count]
+    load_sem, store_sem = refs[3 * count :]
+    loads = [
+        pltpu.make_async_copy(refs[item], held[item], load_sem.at[item]) for item in range(count)
     ]
-    for copy in copies:
-        copy.start()
-    for copy in copies:
-        copy.wait()
+    stores = [
+        pltpu.make_async_copy(held[item], refs[count + item], store_sem.at[item])
+        for item in range(count)
+    ]
+    for load in loads:
+        load.start()
+    for load, store in zip(loads, stores):
+        load.wait()
+        store.start()
+    for store in stores:
+        store.wait()
 
 
 def emit(arrays):
+    any_specs = (pl.BlockSpec(memory_space=pl.ANY),) * len(arrays)
     return pl.pallas_call(
         emit_kernel,
         out_shape=tuple(jax.ShapeDtypeStruct(array.shape, array.dtype) for array in arrays),
-        in_specs=[pl.BlockSpec(memory_space=pltpu.VMEM)] * len(arrays),
-        out_specs=(pl.BlockSpec(memory_space=pl.ANY),) * len(arrays),
-        scratch_shapes=[pltpu.SemaphoreType.DMA((len(arrays),))],
-        compiler_params=pltpu.CompilerParams(vmem_limit_bytes=4 * 1024 * 1024),
+        in_specs=any_specs,
+        out_specs=any_specs,
+        scratch_shapes=[pltpu.VMEM(array.shape, array.dtype) for array in arrays]
+        + [pltpu.SemaphoreType.DMA((len(arrays),))] * 2,
+        compiler_params=pltpu.CompilerParams(vmem_limit_bytes=VMEM_LIMIT),
         name="emit",
     )(*arrays)
 

time: 135 us -> 126 us (0.933)
  Pallas kernels: 130 us -> 125 us
  local copies, waits for them, and re-layouts: 2.84 us -> 0 us
    pallas_call x1, Pallas kernels: 129 us -> 123 us  [run_step(): pl.pallas_call(functools.partial(step_kernel, sizes, 1.0 / math.sqrt(tota...]
    unnamed x6 -> x0, local copies, waits for them, and re-layouts: 2.84 us -> none
where the time goes in v2:
time: 126 us
  Pallas kernels  125 us (99%)
    pallas_call x1, Pallas kernels, run_step(): pl.pallas_call(functools.partial(step_kernel, sizes, 1.0 / math.sqrt(tota...  123 us

profile of v2, /device:TPU:0, one launch (start us, length us, event | category | flops | bytes accessed | tf_op | source)
XLA Modules:
  0.0 125.9 jit_solution(988051036393779721)
XLA Ops:
  0.6 123.1 %step.1 = (bf16[128,2048]{1,0:T(8,128)(2,1)}, f32[3,96,128]{2,1,0:T(8,128)}, f32[3,32,256]{2,1,0:T(8,128)}) custom-call(s32[2]{0:T(128)} %bitcast.11, s32[2]{0:T(128)} %bitcast.12, bf16[2,128,2048]{2,1,0:T(8,128)(2,1)} %bitcast.7, bf16[2,128,2048]{2,1,0:T(8,128)(2,1)} %bitcast.8, bf16[2,128,2048]{2,1,0:T(8,128)(2,1)} %bitcast.9, bf16[128,3072]{1,0:T(8,128)(2,1)} %bitcast.10, ...), custom_call_target="tpu_custom_call" | custom-call | tf_op jit(solution)/shard_map/step/pallas_call | solution.py:662
  123.8 2.0 %emit.1 = (bf16[128,2048]{1,0:T(8,128)(2,1)}, f32[3,96,128]{2,1,0:T(8,128)}, f32[3,32,256]{2,1,0:T(8,128)}) custom-call(bf16[128,2048]{1,0:T(8,128)(2,1)} %get-tuple-element.9.refs_0_, f32[3,96,128]{2,1,0:T(8,128)} %get-tuple-element.10.refs_1_, f32[3,32,256]{2,1,0:T(8,128)} %get-tuple-element.11.refs_2_), custom_call_target="tpu_custom_call" | custom-call | tf_op jit(solution)/shard_map/emit/pallas_call | solution.py:747

commit v3 on v2

--- a/solution.py
+++ b/solution.py
@@ -33,8 +33,12 @@
     return lax.dot_general(left, right, TN, preferred_element_type=jnp.float32)
 
 
-def inner_size(count):
-    return max(size for size in range(1, count + 1) if count % size == 0 and size * size <= count)
+def inner_size(count, dp_count):
+    return max(
+        size
+        for size in range(1, count + 1)
+        if count % size == 0 and dp_count % size == 0 and size * size <= count
+    )
 
 
 def aligned(index, size):
@@ -69,7 +73,10 @@
     hidden_t,
     down_own,
     up_own,
+    rank_line,
     ranks,
+    facts,
+    work_facts,
     weighted,
     weighted_in,
     target,
@@ -119,6 +126,8 @@
     share_recv,
     down_send,
     down_recv,
+    facts_send,
+    facts_recv,
     local_sem,
 ):
     count, inner, dp_count = sizes
@@ -140,17 +149,37 @@
     other = 1 - cfg
     far = me // inner
     near = lax.rem(me, inner)
+    part = lax.rem(dp, inner)
+    bundle = dp // inner
+    bundles = dp_count // inner
+    diagonal = near == part
+    off_diagonal = near != part
     pair = cfg * inner + near
     group = dp * pairs + pair
-    up_group = cfg * dp_count + dp
+    work_block = far * inner + part
     own_rows = aligned(me, tok_here)
+    grid_steps = [(far_step, near_step) for far_step in range(outer) for near_step in range(inner)]
+    up_steps = [
+        (cfg_step, bundle_step, near_step)
+        for cfg_step in range(2)
+        for bundle_step in range(bundles)
+        for near_step in range(inner)
+    ]
     order = (other, cfg)
 
     def head_columns(head):
         return slice(head * HDIM, (head + 1) * HDIM)
 
-    def seq_peer(step):
-        return lax.rem(me + step, count)
+    def when_remote(steps, action):
+        if any(steps):
+            action()
+        else:
+            pl.when(off_diagonal)(action)
+
+    def low_slot(pair_index, dp_index):
+        return (
+            dp_index // inner * inner + lax.rem(pair_index, inner)
+        ) * pairs + pair_index // inner * inner + lax.rem(dp_index, inner)
 
     def device_of(pair_index):
         return {"cfg": pair_index // inner, "seq": far * inner + lax.rem(pair_index, inner)}
@@ -173,9 +202,10 @@
         pltpu.make_async_copy(hidden_ref, hidden_own, local_sem.at[0]),
         pltpu.make_async_copy(down_ref, down_own, local_sem.at[1]),
         pltpu.make_async_copy(
-            up_ref.at[:, :, aligned(me, columns)], up_own, local_sem.at[2]
+            up_ref.at[:, :, aligned(work_block, columns)], up_own, local_sem.at[2]
         ),
-    ] + [
+    ]
+    own_loads = [
         pltpu.make_async_copy(
             fields[member].at[:, :, aligned(me, columns)],
             heads.at[member, 0:2, own_rows, :],
@@ -186,33 +216,43 @@
     for load in loads:
         load.start()
 
+    @pl.when(diagonal)
+    def _():
+        for load in own_loads:
+            load.start()
+
     barrier = pltpu.get_barrier_semaphore()
-    for step in range(1, count):
+    for step in range(1, count * inner):
+        peer_near = lax.rem(near + step // inner % inner, inner)
+        peer_part = lax.rem(part + step % inner, inner)
         pl.semaphore_signal(
-            barrier, inc=1, device_id={"seq": seq_peer(step)}, device_id_type=MESH
+            barrier,
+            inc=1,
+            device_id={
+                "seq": lax.rem(far + step // (inner * inner), outer) * inner + peer_near,
+                "dp": bundle * inner + peer_part,
+            },
+            device_id_type=MESH,
         )
     for step in range(1, groups):
         pl.semaphore_signal(barrier, inc=1, device_id=group_device(step), device_id_type=MESH)
-    def field_copy(phase, head, member, step):
-        peer = seq_peer(step)
+
+    def field_copy(phase, head, member, steps):
+        peer_far = lax.rem(far + steps[0], outer)
+        peer_part = lax.rem(near + steps[1], inner)
         half = order[phase]
-        start = pl.multiple_of(peer * columns, columns) + head * HDIM
+        start = pl.multiple_of((peer_far * inner + peer_part) * columns, columns) + head * HDIM
         return remote(
             fields[member].at[half, :, pl.ds(start, HDIM)],
             heads.at[member, half, own_rows, head_columns(head)],
-            field_send.at[phase, head, member, step],
-            field_recv.at[phase, head, member, step],
-            {"seq": peer},
-        )
-
-    def start_fields(phase, head, member):
-        for step in range(1, count):
-            field_copy(phase, head, member, step).start()
-
-    def wait_fields(phase, head):
-        for member in (1, 2, 0):
-            for step in range(1, count):
-                field_copy(phase, head, member, step).wait_recv()
+            field_send.at[phase, head, member, *steps],
+            field_recv.at[phase, head, member, *steps],
+            {"seq": peer_far * inner + part, "dp": bundle * inner + peer_part},
+        )
+
+    def each_field(phase, head, member, action):
+        for steps in grid_steps:
+            when_remote(steps, getattr(field_copy(phase, head, member, steps), action))
 
     def pass_copy(head, member):
         return remote(
@@ -225,7 +265,7 @@
 
     def rank_copy(way, hop):
         toward, back_by = (1, outer - hop) if way == 0 else (outer - 1, hop)
-        block = ranks.at[lax.rem(far + back_by, outer), near]
+        block = rank_line.at[lax.rem(far + back_by, outer)]
         return remote(
             block,
             block,
@@ -250,12 +290,22 @@
                 getattr(rank_copy(way, hop), action)()
 
     def fan_copy(step):
-        return remote(
-            ranks.at[:, near],
+        peer_part = lax.rem(near + step, inner)
+        return remote(
+            rank_line,
             ranks.at[:, near],
             fan_send.at[step],
             fan_recv.at[step],
-            {"seq": far * inner + lax.rem(near + step, inner)},
+            {"seq": far * inner + part, "dp": bundle * inner + peer_part},
+        )
+
+    def facts_copy(step):
+        return remote(
+            facts,
+            work_facts,
+            facts_send.at[step],
+            facts_recv.at[0],
+            {"dp": bundle * inner + lax.rem(part + step, inner)},
         )
 
     def swap_copy(head):
@@ -267,16 +317,20 @@
             {"cfg": other},
         )
 
-    def out_copy(head, step):
-        peer = seq_peer(step)
-        start = pl.multiple_of(me * columns, columns) + head * HDIM
+    def out_copy(head, steps):
+        peer = lax.rem(far + steps[0], outer) * inner + lax.rem(part + steps[1], inner)
+        start = pl.multiple_of(work_block * columns, columns) + head * HDIM
         return remote(
             student.at[aligned(peer, tok_here), head_columns(head)],
             tokens_ref.at[:, pl.ds(start, HDIM)],
-            out_send.at[head, step],
-            out_recv.at[head, step],
-            {"seq": peer},
-        )
+            out_send.at[head, *steps],
+            out_recv.at[head, *steps],
+            {"seq": peer, "dp": bundle * inner + near},
+        )
+
+    def each_out(head, action):
+        for steps in grid_steps:
+            when_remote(steps, getattr(out_copy(head, steps), action))
 
     def cols_copy(step):
         return remote(
@@ -287,25 +341,30 @@
             group_device(step),
         )
 
-    def up_copy(step):
-        peer = lax.rem(up_group + step, up_groups)
-        return remote(
-            up_parts.at[peer],
-            up_in.at[step],
-            up_send.at[step],
-            up_recv.at[step],
-            {"cfg": peer // dp_count, "dp": lax.rem(peer, dp_count)},
-        )
+    def up_copy(steps):
+        peer_cfg = lax.rem(cfg + steps[0], 2)
+        peer_dp = lax.rem(bundle + steps[1], bundles) * inner + lax.rem(near + steps[2], inner)
+        return remote(
+            up_parts.at[peer_cfg * dp_count + peer_dp],
+            up_in.at[steps],
+            up_send.at[steps],
+            up_recv.at[steps],
+            {"cfg": peer_cfg, "seq": work_block, "dp": peer_dp},
+        )
+
+    def each_up(action):
+        for steps in up_steps:
+            when_remote(steps, getattr(up_copy(steps), action))
 
     def near_copy(member, far_step, step):
-        peer = lax.rem(near + step, inner)
+        peer = lax.rem(part + step, inner)
         row = lax.rem(far + far_step, outer)
         return remote(
             back.at[aligned(row * inner + peer, tok_here), head_columns(member)],
             near_in.at[far_step, step, :, head_columns(member)],
             near_send.at[member, far_step, step],
             near_recv.at[member, far_step, step],
-            {"seq": far * inner + peer},
+            {"dp": bundle * inner + peer},
         )
 
     def far_copy(member, step):
@@ -320,7 +379,7 @@
     def low_copy(member, step):
         return remote(
             low.at[:, head_columns(member)],
-            low_all.at[group, :, head_columns(member)],
+            low_all.at[low_slot(pair, dp), :, head_columns(member)],
             low_send.at[member, step],
             low_recv.at[member, step],
             device_of(lax.rem(pair + step, pairs)),
@@ -329,7 +388,7 @@
     def share_copy(member, pair_step, step):
         source = lax.rem(pair - pair_step + pairs, pairs)
         lanes = head_columns(member)
-        slot = low_all.at[dp * pairs + source, :, lanes]
+        slot = low_all.at[low_slot(source, dp), :, lanes]
         return remote(
             low.at[:, lanes] if pair_step == 0 else slot,
             slot,
@@ -351,39 +410,53 @@
     def guide_scale(half):
         return 1.0 + 0.5 * guide_ref[half].astype(jnp.float32)
 
-    def weighting(half):
-        scale = guide_scale(half)
-        return jnp.where(cfg == 0, scale, 1.0 - scale)
-
     rank_index = (lax.broadcasted_iota(jnp.int32, (1, ADAPTER_RANK), 1) + 1).astype(jnp.float32)
     time_frac = (time_ref[cfg].astype(jnp.float32) + 0.5) / TSTEPS
     modulation = 1.0 + 0.5 * jnp.cos(
         math.pi * rank_index * time_frac + 0.25 * rank_index * guide_scale(cfg)
     )
 
+    facts[0] = modulation
+    for half in range(2):
+        facts[1 + half] = jnp.full((1, ADAPTER_RANK), guide_scale(half), jnp.float32)
+
+    def weighting(half):
+        scale = work_facts[1 + half]
+        return jnp.where(cfg == 0, scale, 1.0 - scale)
+
     phases = [(phase, head) for phase in range(2) for head in range(heads_here)]
+    sends = [(phase, head, member) for phase, head in phases for member in (1, 2, 0)]
+    pl.semaphore_wait(barrier, count * inner + groups - 2)
+    each_field(*sends[0], "start")
+
+    @pl.when(diagonal)
+    def _():
+        work_facts[...] = facts[...]
+        for step in range(1, inner):
+            facts_copy(step).start()
+
     loads[0].wait()
     loads[1].wait()
     for member in range(3):
         projected = dot_f32(hidden_own[...], down_own[member]) * modulation
-        ranks[far, near, :, head_columns(member)] = projected.astype(jnp.bfloat16)
-    pl.semaphore_wait(barrier, count + groups - 2)
-
-    sends = [(phase, head, member) for phase, head in phases for member in (1, 2, 0)]
-    sent = 0
+        rank_line[far, :, head_columns(member)] = projected.astype(jnp.bfloat16)
     for hop in range(outer - 1):
-        if hop > 0:
-            rank_step(hop - 1, "wait_recv", ranks_come)
         rank_step(hop, "start", ranks_leave)
-        start_fields(*sends[sent])
-        sent += 1
-    for turn in sends[sent : 2 * sent]:
-        start_fields(*turn)
-    rank_step(outer - 2, "wait_recv", ranks_come)
-    for step in range(1, inner):
-        fan_copy(step).start()
-    for turn in sends[2 * sent :]:
-        start_fields(*turn)
+        each_field(*sends[1 + hop], "start")
+        rank_step(hop, "wait_recv", ranks_come)
+    for step in range(inner):
+        when_remote((step,), fan_copy(step).start)
+    for turn in sends[outer:]:
+        each_field(*turn, "start")
+
+    @pl.when(diagonal)
+    def _():
+        ranks[:, near] = rank_line[...]
+
+    @pl.when(off_diagonal)
+    def _():
+        facts_copy(inner - 1).wait_recv()
+
     rows_here = hidden_cols.shape[2] // outer
     for block in range(outer * groups):
         target_dp = block % dp_count
@@ -396,8 +469,12 @@
     hidden_all[group] = hidden_cols[group]
     for step in range(1, groups):
         cols_copy(step).start()
-    for load in loads[2:]:
-        load.wait()
+    loads[2].wait()
+
+    @pl.when(diagonal)
+    def _():
+        for load in own_loads:
+            load.wait()
 
     far_order = sorted(range(outer), key=lambda step: (step == 0, abs(2 * step - outer)))
 
@@ -424,12 +501,9 @@
         run_blocks(one_block)
 
     for head in range(heads_here):
-        wait_fields(0, head)
-
-        @pl.when(cfg == 0)
-        def _():
-            for member in range(3):
-                pass_copy(head, member).start()
+        for member in (1, 2, 0):
+            each_field(0, head, member, "wait_recv")
+            pl.when(cfg == 0)(pass_copy(head, member).start)
 
         def store_other(rows, attended):
             weighted[head, rows, :] = (weighting(other) * attended).astype(jnp.bfloat16)
@@ -437,12 +511,13 @@
         teacher(other, head, store_other)
         swap_copy(head).start()
 
-    for step in range(1, inner):
-        fan_copy(step).wait_recv()
+    for step in range(inner):
+        when_remote((step,), fan_copy(step).wait_recv)
 
     for head in range(heads_here):
         lanes = head_columns(head)
-        wait_fields(1, head)
+        for member in (1, 2, 0):
+            each_field(1, head, member, "wait_recv")
 
         def store_own(rows, attended):
             target[rows, :] = weighting(cfg) * attended
@@ -486,8 +561,7 @@
 
         run_blocks(one_block)
         if head < heads_here - 1:
-            for step in range(1, count):
-                out_copy(head, step).start()
+            each_out(head, "start")
 
         gradients = (
             grad_query[...],
@@ -495,30 +569,33 @@
             grad_value[...].astype(jnp.bfloat16),
         )
         for member, gradient in enumerate(gradients):
-            part = dot_nt(gradient, up_own[member, :, lanes])
+            piece = dot_nt(gradient, up_own[member, :, lanes])
             if head > 0:
-                part = part + back_sum[:, head_columns(member)]
+                piece = piece + back_sum[:, head_columns(member)]
             if head < heads_here - 1:
-                back_sum[:, head_columns(member)] = part
+                back_sum[:, head_columns(member)] = piece
             else:
-                back[:, head_columns(member)] = part.astype(jnp.bfloat16)
+                back[:, head_columns(member)] = piece.astype(jnp.bfloat16)
                 for far_step in far_order:
                     for step in range(1, inner):
                         near_copy(member, far_step, step).start()
         if head == heads_here - 1:
-            for step in range(1, count):
-                out_copy(head, step).start()
+            each_out(head, "start")
         for member, gradient in enumerate(gradients):
             low_rank = ranks[:, :, :, head_columns(member)].reshape(length, ADAPTER_RANK)
-            part = dot_tn(low_rank, gradient).astype(jnp.bfloat16)
-            up_parts[:, member, :, lanes] = part.reshape(up_groups, -1, HDIM)
-
-    for step in range(1, up_groups):
-        up_copy(step).start()
+            piece = dot_tn(low_rank, gradient).astype(jnp.bfloat16)
+            up_parts[:, member, :, lanes] = piece.reshape(up_groups, -1, HDIM)
+
+    each_up("start")
     own_store = pltpu.make_async_copy(
         student.at[own_rows, :], tokens_ref.at[:, aligned(me, columns)], local_sem.at[6]
     )
-    own_store.start()
+
+    @pl.when(diagonal)
+    def _():
+        own_store.start()
+        up_in[0, 0, 0] = up_parts[cfg * dp_count + dp]
+
     for step in range(1, groups):
         cols_copy(step).wait_recv()
     gathered_cols = hidden_all[...].reshape(groups * tok_here, -1)
@@ -529,23 +606,23 @@
         lanes = head_columns(member)
         for far_step in far_order:
             row = lax.rem(far + far_step, outer)
-            part = back[aligned(row * inner + near, tok_here), lanes].astype(jnp.float32)
+            total = back[aligned(row * inner + part, tok_here), lanes].astype(jnp.float32)
             for step in range(1, inner):
                 near_copy(member, far_step, step).wait_recv()
-                part = part + near_in[far_step, step, :, lanes].astype(jnp.float32)
+                total = total + near_in[far_step, step, :, lanes].astype(jnp.float32)
             if far_step > 0:
-                far_out[far_step, :, lanes] = part.astype(jnp.bfloat16)
+                far_out[far_step, :, lanes] = total.astype(jnp.bfloat16)
                 far_copy(member, far_step).start()
-        return part
+        return total
 
     def reduce_far(member, total):
         lanes = head_columns(member)
         for step in range(1, outer):
             far_copy(member, step).wait_recv()
             total = total + far_in[step, :, lanes].astype(jnp.float32)
-        low_grad = (total * modulation).astype(jnp.bfloat16)
+        low_grad = (total * work_facts[0]).astype(jnp.bfloat16)
         low[:, lanes] = low_grad
-        low_all[group, :, lanes] = low_grad
+        low_all[low_slot(pair, dp), :, lanes] = low_grad
         for step in range(1, pairs):
             low_copy(member, step).start()
         for step in range(1, dp_count):
@@ -580,10 +657,10 @@
         if turn >= 3:
             contract(turn - 3)
 
-    up_total = up_parts[up_group].astype(jnp.float32)
-    for step in range(1, up_groups):
-        up_copy(step).wait_recv()
-        up_total = up_total + up_in[step].astype(jnp.float32)
+    each_up("wait_recv")
+    up_total = up_in[up_steps[0]].astype(jnp.float32)
+    for steps in up_steps[1:]:
+        up_total = up_total + up_in[steps].astype(jnp.float32)
     grad_up_ref[...] = up_total
 
     for member in range(3):
@@ -594,11 +671,14 @@
             down_total = down_total + down_in[step, :, lanes].astype(jnp.float32)
         grad_down_ref[member] = down_total
 
-    own_store.wait()
-    for phase, head in phases:
-        for member in range(3):
-            for step in range(1, count):
-                field_copy(phase, head, member, step).wait_send()
+    @pl.when(diagonal)
+    def _():
+        own_store.wait()
+        for step in range(1, inner):
+            facts_copy(step).wait_send()
+
+    for turn in sends:
+        each_field(*turn, "wait_send")
     for head in range(heads_here):
         swap_copy(head).wait_send()
 
@@ -607,16 +687,14 @@
             for member in range(3):
                 pass_copy(head, member).wait_send()
 
-        for step in range(1, count):
-            out_copy(head, step).wait()
+        each_out(head, "wait")
     for hop in range(outer - 1):
         rank_step(hop, "wait_send", ranks_leave)
-    for step in range(1, inner):
-        fan_copy(step).wait_send()
+    for step in range(inner):
+        when_remote((step,), fan_copy(step).wait_send)
     for step in range(1, groups):
         cols_copy(step).wait_send()
-    for step in range(1, up_groups):
-        up_copy(step).wait_send()
+    each_up("wait_send")
     for member in range(3):
         for pair_step in range(pairs):
             if pair_step > 0:
@@ -676,7 +754,10 @@
             bf16(group_cols, groups * tok_here),
             bf16(3, model_width, ADAPTER_RANK),
             bf16(3, ADAPTER_RANK, columns),
+            bf16(outer, tok_here, rank_cols),
             bf16(outer, inner, tok_here, rank_cols),
+            f32(3, 1, ADAPTER_RANK),
+            f32(3, 1, ADAPTER_RANK),
             bf16(heads_here, length, HDIM),
             bf16(heads_here, length, HDIM),
             f32(length, HDIM),
@@ -695,24 +776,25 @@
             bf16(outer, tok_here, rank_cols),
             bf16(length, columns),
             bf16(up_groups, 3, up_rows, columns),
-            bf16(up_groups, 3, up_rows, columns),
+            bf16(2, dp_count // inner, inner, 3, up_rows, columns),
             bf16(tok_here, rank_cols),
             bf16(groups, tok_here, rank_cols),
             bf16(outer, down_rows, rank_cols),
             bf16(outer, down_rows, rank_cols),
-            *sems(2, heads_here, 3, count),
+            *sems(2, heads_here, 3, outer, inner),
             *sems(heads_here, 3),
             *sems(2, outer),
             *sems(inner),
             *sems(heads_here),
-            *sems(heads_here, count),
+            *sems(heads_here, outer, inner),
             *sems(groups),
-            *sems(up_groups),
+            *sems(2, dp_count // inner, inner),
             *sems(3, outer, inner),
             *sems(3, outer),
             *sems(3, pairs),
             *sems(3, pairs, dp_count),
             *sems(3, outer),
+            *sems(inner),
             pltpu.SemaphoreType.DMA((7,)),
         ],
         compiler_params=pltpu.CompilerParams(
@@ -767,8 +849,9 @@
     timestep_index,
 ):
     seq_count = lax.axis_size("seq")
+    dp_count = lax.axis_size("dp")
     outputs = run_step(
-        (seq_count, inner_size(seq_count), lax.axis_size("dp")),
+        (seq_count, inner_size(seq_count, dp_count), dp_count),
         guidance_index[:, 0],
         timestep_index[:, 0],
         (teacher_query[0, :, 0], teacher_key[0, :, 0], teacher_value[0, :, 0]),

time: 126 us -> 126 us (level)
  no operation moved by 1% of the time
where the time goes in v3:
time: 126 us
  Pallas kernels  125 us (99%)
    pallas_call x1, Pallas kernels, run_step(): pl.pallas_call(functools.partial(step_kernel, sizes, 1.0 / math.sqrt(tota...  123 us

profile of v3, /device:TPU:0, one launch (start us, length us, event | category | flops | bytes accessed | tf_op | source)
XLA Modules:
  0.0 125.5 jit_solution(16474339841344593058)
XLA Ops:
  0.6 122.8 %step.1 = (bf16[128,2048]{1,0:T(8,128)(2,1)}, f32[3,96,128]{2,1,0:T(8,128)}, f32[3,32,256]{2,1,0:T(8,128)}) custom-call(s32[2]{0:T(128)} %bitcast.11, s32[2]{0:T(128)} %bitcast.12, bf16[2,128,2048]{2,1,0:T(8,128)(2,1)} %bitcast.7, bf16[2,128,2048]{2,1,0:T(8,128)(2,1)} %bitcast.8, bf16[2,128,2048]{2,1,0:T(8,128)(2,1)} %bitcast.9, bf16[128,3072]{1,0:T(8,128)(2,1)} %bitcast.10, ...), custom_call_target="tpu_custom_call" | custom-call | tf_op jit(solution)/shard_map/step/pallas_call | solution.py:740
  123.4 2.0 %emit.1 = (bf16[128,2048]{1,0:T(8,128)(2,1)}, f32[3,96,128]{2,1,0:T(8,128)}, f32[3,32,256]{2,1,0:T(8,128)}) custom-call(bf16[128,2048]{1,0:T(8,128)(2,1)} %get-tuple-element.9.refs_0_, f32[3,96,128]{2,1,0:T(8,128)} %get-tuple-element.10.refs_1_, f32[3,32,256]{2,1,0:T(8,128)} %get-tuple-element.11.refs_2_), custom_call_target="tpu_custom_call" | custom-call | tf_op jit(solution)/shard_map/emit/pallas_call | solution.py:829

commit v4 on v3

--- a/solution.py
+++ b/solution.py
@@ -13,8 +13,10 @@
 TSTEPS = 1000
 FACTOR = HDIM ** (-0.5)
 FACTOR_BASE2 = FACTOR * math.log2(math.e)
-VMEM_LIMIT = 60 * 1024 * 1024
+VMEM_LIMIT = 63 * 1024 * 1024
 BLOCK = 512
+BLOCK_AREA = BLOCK * 1024
+KEPT_BYTES = 16 * 1024 * 1024
 MESH = pl.DeviceIdType.MESH
 
 NT = (((1,), (1,)), ((), ()))
@@ -88,6 +90,9 @@
     grad_query,
     grad_key,
     grad_value,
+    teacher_w,
+    student_w,
+    student_p,
     back_sum,
     back,
     near_in,
@@ -140,7 +145,7 @@
     length = tok_here * count
     columns = student.shape[1]
     heads_here = columns // HDIM
-    step_rows = min(BLOCK, length)
+    step_rows = min(BLOCK, BLOCK_AREA // length, length)
     blocks = length // step_rows
 
     me = lax.axis_index("seq")
@@ -425,7 +430,7 @@
         return jnp.where(cfg == 0, scale, 1.0 - scale)
 
     phases = [(phase, head) for phase in range(2) for head in range(heads_here)]
-    sends = [(phase, head, member) for phase, head in phases for member in (1, 2, 0)]
+    sends = [(phase, head, member) for phase, head in phases for member in (1, 0, 2)]
     pl.semaphore_wait(barrier, count * inner + groups - 2)
     each_field(*sends[0], "start")
 
@@ -488,27 +493,52 @@
 
         lax.fori_loop(0, blocks // unroll, some, 0)
 
-    def teacher(half, head, store):
+    def block_rows(step):
+        return aligned(step, step_rows)
+
+    def teacher_weights(half, lanes):
+        def one_block(step):
+            probability = probs_by_key(
+                heads[1, half, :, lanes], heads[0, half, block_rows(step), lanes]
+            )
+            teacher_w[step] = probability.astype(jnp.bfloat16)
+
+        run_blocks(one_block)
+
+    def student_weights(step):
+        if student_w is None:
+            return student_p[step].astype(jnp.bfloat16)
+        return student_w[step]
+
+    def arrived(phase, head, member):
+        each_field(phase, head, member, "wait_recv")
+        if phase == 0:
+            pl.when(cfg == 0)(pass_copy(head, member).start)
+
+    def project(head, member, projected):
         lanes = head_columns(head)
-        value_t[...] = heads[2, half, :, lanes].T
+        pl.when(cfg == 1)(pass_copy(head, member).wait_recv)
+        low_rank = ranks[:, :, :, head_columns(member)].reshape(length, ADAPTER_RANK)
+        frozen = heads[member, 2 * cfg, :, lanes].astype(jnp.float32)
+        projected[...] = (frozen + dot_f32(low_rank, up_own[member, :, lanes])).astype(
+            jnp.bfloat16
+        )
+
+    for head in range(heads_here):
+        lanes = head_columns(head)
+        arrived(0, head, 1)
+        arrived(0, head, 0)
+        teacher_weights(other, lanes)
+        arrived(0, head, 2)
+        value_t[...] = heads[2, other, :, lanes].T
 
         def one_block(step):
-            rows = aligned(step, step_rows)
-            weights = probs_by_key(heads[1, half, :, lanes], heads[0, half, rows, lanes])
-            attended = dot_f32(value_t[...], weights.astype(jnp.bfloat16)).T
-            store(rows, attended.astype(jnp.bfloat16).astype(jnp.float32))
+            attended = dot_f32(value_t[...], teacher_w[step]).T.astype(jnp.bfloat16)
+            weighted[head, block_rows(step), :] = (
+                weighting(other) * attended.astype(jnp.float32)
+            ).astype(jnp.bfloat16)
 
         run_blocks(one_block)
-
-    for head in range(heads_here):
-        for member in (1, 2, 0):
-            each_field(0, head, member, "wait_recv")
-            pl.when(cfg == 0)(pass_copy(head, member).start)
-
-        def store_other(rows, attended):
-            weighted[head, rows, :] = (weighting(other) * attended).astype(jnp.bfloat16)
-
-        teacher(other, head, store_other)
         swap_copy(head).start()
 
     for step in range(inner):
@@ -516,52 +546,57 @@
 
     for head in range(heads_here):
         lanes = head_columns(head)
-        for member in (1, 2, 0):
-            each_field(1, head, member, "wait_recv")
-
-        def store_own(rows, attended):
-            target[rows, :] = weighting(cfg) * attended
-
-        teacher(cfg, head, store_own)
-
-        @pl.when(cfg == 1)
-        def _():
-            for member in range(3):
-                pass_copy(head, member).wait_recv()
-
-        for member, projected in enumerate((s_query, s_key, s_value)):
-            low_rank = ranks[:, :, :, head_columns(member)].reshape(length, ADAPTER_RANK)
-            frozen = heads[member, 2 * cfg, :, lanes].astype(jnp.float32)
-            projected[...] = (frozen + dot_f32(low_rank, up_own[member, :, lanes])).astype(
-                jnp.bfloat16
-            )
+        arrived(1, head, 1)
+        project(head, 1, s_key)
         key_t[...] = s_key[...].T
-        value_t[...] = s_value[...].T
+        arrived(1, head, 0)
+        project(head, 0, s_query)
+        teacher_weights(cfg, lanes)
+
+        def one_block(step):
+            probability = probs_by_key(s_key[...], s_query[block_rows(step), :])
+            student_p[step] = probability
+            if student_w is not None:
+                student_w[step] = probability.astype(jnp.bfloat16)
+
+        run_blocks(one_block)
         grad_key[...] = jnp.zeros_like(grad_key)
         grad_value[...] = jnp.zeros_like(grad_value)
+        arrived(1, head, 2)
+        project(head, 2, s_value)
+        value_t[...] = s_value[...].T
+
+        def one_block(step):
+            attended = dot_f32(value_t[...], student_weights(step)).T
+            student[block_rows(step), lanes] = attended.astype(jnp.bfloat16)
+
+        run_blocks(one_block)
+        each_out(head, "start")
+        value_t[...] = heads[2, cfg, :, lanes].T
+
+        def one_block(step):
+            attended = dot_f32(value_t[...], teacher_w[step]).T.astype(jnp.bfloat16)
+            target[block_rows(step), :] = weighting(cfg) * attended.astype(jnp.float32)
+
+        run_blocks(one_block)
         swap_copy(head).wait_recv()
 
         def one_block(step):
-            rows = aligned(step, step_rows)
-            query_block = s_query[rows, :]
-            probability = probs_by_key(s_key[...], query_block)
-            weights = probability.astype(jnp.bfloat16)
-            attended = dot_f32(value_t[...], weights).T.astype(jnp.bfloat16)
-            student[rows, lanes] = attended
+            rows = block_rows(step)
+            probability = student_p[step]
             aim = target[rows, :] + weighted_in[head, rows, :].astype(jnp.float32)
-            upstream = ((attended.astype(jnp.float32) - aim) * out_scale).astype(jnp.bfloat16)
-            grad_value[...] += dot_f32(weights, upstream)
+            error = student[rows, lanes].astype(jnp.float32) - aim
+            upstream = (error * out_scale).astype(jnp.bfloat16)
+            grad_value[...] += dot_f32(student_weights(step), upstream)
             prob_grad = dot_nt(s_value[...], upstream)
             center = jnp.sum(probability * prob_grad, axis=0, keepdims=True)
             score_grad = (probability * (prob_grad - center)).astype(jnp.bfloat16)
-            grad_key[...] += dot_f32(score_grad, query_block)
+            grad_key[...] += dot_f32(score_grad, s_query[rows, :])
             grad_query[rows, :] = (dot_f32(key_t[...], score_grad).T * FACTOR).astype(
                 jnp.bfloat16
             )
 
         run_blocks(one_block)
-        if head < heads_here - 1:
-            each_out(head, "start")
 
         gradients = (
             grad_query[...],
@@ -579,8 +614,6 @@
                 for far_step in far_order:
                     for step in range(1, inner):
                         near_copy(member, far_step, step).start()
-        if head == heads_here - 1:
-            each_out(head, "start")
         for member, gradient in enumerate(gradients):
             low_rank = ranks[:, :, :, head_columns(member)].reshape(length, ADAPTER_RANK)
             piece = dot_tn(low_rank, gradient).astype(jnp.bfloat16)
@@ -596,11 +629,12 @@
         own_store.start()
         up_in[0, 0, 0] = up_parts[cfg * dp_count + dp]
 
-    for step in range(1, groups):
-        cols_copy(step).wait_recv()
-    gathered_cols = hidden_all[...].reshape(groups * tok_here, -1)
-    hidden_t[...] = gathered_cols.T
-    down_rows = gathered_cols.shape[1] // outer
+    down_rows = hidden_t.shape[0] // outer
+
+    def gather_columns():
+        for step in range(1, groups):
+            cols_copy(step).wait_recv()
+        hidden_t[...] = hidden_all[...].reshape(groups * tok_here, -1).T
 
     def reduce_near(member):
         lanes = head_columns(member)
@@ -652,6 +686,8 @@
             totals[turn] = reduce_near(turn)
         if 1 <= turn < 4:
             reduce_far(turn - 1, totals[turn - 1])
+        if turn == 1:
+            gather_columns()
         if 2 <= turn < 5:
             spread(turn - 2)
         if turn >= 3:
@@ -709,6 +745,14 @@
                 near_copy(member, far_step, step).wait_send()
 
 
+def with_gaps(kernel, scratch, skipped):
+    def filled(*refs):
+        held = iter(refs[skipped:])
+        kernel(*refs[:skipped], *[None if item is None else next(held) for item in scratch])
+
+    return filled
+
+
 def run_step(sizes, guide, time_index, fields, hidden, down, up):
     count, inner, dp_count = sizes
     outer = count // inner
@@ -719,6 +763,7 @@
     model_width = hidden.shape[1]
     length, columns = tok_here * count, width // count
     heads_here = columns // HDIM
+    step_rows = min(BLOCK, BLOCK_AREA // length, length)
     rank_cols = 3 * ADAPTER_RANK
     group_cols = model_width // groups
     down_rows = group_cols // outer
@@ -737,8 +782,63 @@
         return [pltpu.SemaphoreType.DMA(shape)] * 2
 
     total_rows = 2 * dp_count * length
+    keep_weights = 8 * length * length <= KEPT_BYTES
+    scratch = [
+        bf16(3, 3, length, columns),
+        bf16(tok_here, model_width),
+        bf16(groups, tok_here, group_cols),
+        bf16(groups, tok_here, group_cols),
+        bf16(group_cols, groups * tok_here),
+        bf16(3, model_width, ADAPTER_RANK),
+        bf16(3, ADAPTER_RANK, columns),
+        bf16(outer, tok_here, rank_cols),
+        bf16(outer, inner, tok_here, rank_cols),
+        f32(3, 1, ADAPTER_RANK),
+        f32(3, 1, ADAPTER_RANK),
+        bf16(heads_here, length, HDIM),
+        bf16(heads_here, length, HDIM),
+        f32(length, HDIM),
+        bf16(length, HDIM),
+        bf16(length, HDIM),
+        bf16(length, HDIM),
+        bf16(HDIM, length),
+        bf16(HDIM, length),
+        bf16(length, HDIM),
+        f32(length, HDIM),
+        f32(length, HDIM),
+        bf16(length // step_rows, length, step_rows),
+        bf16(length // step_rows, length, step_rows) if keep_weights else None,
+        f32(length // step_rows, length, step_rows),
+        f32(length, rank_cols) if heads_here > 1 else None,
+        bf16(length, rank_cols),
+        bf16(outer, inner, tok_here, rank_cols),
+        bf16(outer, tok_here, rank_cols),
+        bf16(outer, tok_here, rank_cols),
+        bf16(length, columns),
+        bf16(up_groups, 3, up_rows, columns),
+        bf16(2, dp_count // inner, inner, 3, up_rows, columns),
+        bf16(tok_here, rank_cols),
+        bf16(groups, tok_here, rank_cols),
+        bf16(outer, down_rows, rank_cols),
+        bf16(outer, down_rows, rank_cols),
+        *sems(2, heads_here, 3, outer, inner),
+        *sems(heads_here, 3),
+        *sems(2, outer),
+        *sems(inner),
+        *sems(heads_here),
+        *sems(heads_here, outer, inner),
+        *sems(groups),
+        *sems(2, dp_count // inner, inner),
+        *sems(3, outer, inner),
+        *sems(3, outer),
+        *sems(3, pairs),
+        *sems(3, pairs, dp_count),
+        *sems(3, outer),
+        *sems(inner),
+        pltpu.SemaphoreType.DMA((7,)),
+    ]
     return pl.pallas_call(
-        functools.partial(step_kernel, sizes, 1.0 / math.sqrt(total_rows)),
+        with_gaps(functools.partial(step_kernel, sizes, 1.0 / math.sqrt(total_rows)), scratch, 11),
         out_shape=(
             jax.ShapeDtypeStruct((tok_here, width), jnp.bfloat16),
             jax.ShapeDtypeStruct((3, down_rows, ADAPTER_RANK), jnp.float32),
@@ -746,57 +846,7 @@
         ),
         in_specs=[smem_spec] * 2 + [any_spec] * 6,
         out_specs=(any_spec, vmem_spec, vmem_spec),
-        scratch_shapes=[
-            bf16(3, 3, length, columns),
-            bf16(tok_here, model_width),
-            bf16(groups, tok_here, group_cols),
-            bf16(groups, tok_here, group_cols),
-            bf16(group_cols, groups * tok_here),
-            bf16(3, model_width, ADAPTER_RANK),
-            bf16(3, ADAPTER_RANK, columns),
-            bf16(outer, tok_here, rank_cols),
-            bf16(outer, inner, tok_here, rank_cols),
-            f32(3, 1, ADAPTER_RANK),
-            f32(3, 1, ADAPTER_RANK),
-            bf16(heads_here, length, HDIM),
-            bf16(heads_here, length, HDIM),
-            f32(length, HDIM),
-            bf16(length, HDIM),
-            bf16(length, HDIM),
-            bf16(length, HDIM),
-            bf16(HDIM, length),
-            bf16(HDIM, length),
-            bf16(length, HDIM),
-            f32(length, HDIM),
-            f32(length, HDIM),
-            f32(length, rank_cols),
-            bf16(length, rank_cols),
-            bf16(outer, inner, tok_here, rank_cols),
-            bf16(outer, tok_here, rank_cols),
-            bf16(outer, tok_here, rank_cols),
-            bf16(length, columns),
-            bf16(up_groups, 3, up_rows, columns),
-            bf16(2, dp_count // inner, inner, 3, up_rows, columns),
-            bf16(tok_here, rank_cols),
-            bf16(groups, tok_here, rank_cols),
-            bf16(outer, down_rows, rank_cols),
-            bf16(outer, down_rows, rank_cols),
-            *sems(2, heads_here, 3, outer, inner),
-            *sems(heads_here, 3),
-            *sems(2, outer),
-            *sems(inner),
-            *sems(heads_here),
-            *sems(heads_here, outer, inner),
-            *sems(groups),
-            *sems(2, dp_count // inner, inner),
-            *sems(3, outer, inner),
-            *sems(3, outer),
-            *sems(3, pairs),
-            *sems(3, pairs, dp_count),
-            *sems(3, outer),
-            *sems(inner),
-            pltpu.SemaphoreType.DMA((7,)),
-        ],
+        scratch_shapes=[item for item in scratch if item is not None],
         compiler_params=pltpu.CompilerParams(
             collective_id=0, has_side_effects=True, vmem_limit_bytes=VMEM_LIMIT
         ),

time: 126 us -> 120 us (0.952)
  Pallas kernels: 125 us -> 119 us
    pallas_call x1, Pallas kernels: 123 us -> 117 us  [run_step(): pl.pallas_call(with_gaps(functools.partial(step_kernel, sizes, 1.0 / math...]
where the time goes in v4:
time: 120 us
  Pallas kernels  119 us (99%)
    pallas_call x1, Pallas kernels, run_step(): pl.pallas_call(with_gaps(functools.partial(step_kernel, sizes, 1.0 / math...  117 us

profile of v4, /device:TPU:0, one launch (start us, length us, event | category | flops | bytes accessed | tf_op | source)
XLA Modules:
  0.0 120.0 jit_solution(5736038902600623277)
XLA Ops:
  0.6 117.2 %step.1 = (bf16[128,2048]{1,0:T(8,128)(2,1)}, f32[3,96,128]{2,1,0:T(8,128)}, f32[3,32,256]{2,1,0:T(8,128)}) custom-call(s32[2]{0:T(128)} %bitcast.11, s32[2]{0:T(128)} %bitcast.12, bf16[2,128,2048]{2,1,0:T(8,128)(2,1)} %bitcast.7, bf16[2,128,2048]{2,1,0:T(8,128)(2,1)} %bitcast.8, bf16[2,128,2048]{2,1,0:T(8,128)(2,1)} %bitcast.9, bf16[128,3072]{1,0:T(8,128)(2,1)} %bitcast.10, ...), custom_call_target="tpu_custom_call" | custom-call | tf_op jit(solution)/shard_map/step/pallas_call | solution.py:840
  117.9 2.0 %emit.1 = (bf16[128,2048]{1,0:T(8,128)(2,1)}, f32[3,96,128]{2,1,0:T(8,128)}, f32[3,32,256]{2,1,0:T(8,128)}) custom-call(bf16[128,2048]{1,0:T(8,128)(2,1)} %get-tuple-element.9.refs_0_, f32[3,96,128]{2,1,0:T(8,128)} %get-tuple-element.10.refs_1_, f32[3,32,256]{2,1,0:T(8,128)} %get-tuple-element.11.refs_2_), custom_call_target="tpu_custom_call" | custom-call | tf_op jit(solution)/shard_map/emit/pallas_call | solution.py:879

commit v5 on v4

--- a/solution.py
+++ b/solution.py
@@ -87,6 +87,7 @@
     s_value,
     key_t,
     value_t,
+    upstream,
     grad_query,
     grad_key,
     grad_value,
@@ -544,98 +545,6 @@
     for step in range(inner):
         when_remote((step,), fan_copy(step).wait_recv)
 
-    for head in range(heads_here):
-        lanes = head_columns(head)
-        arrived(1, head, 1)
-        project(head, 1, s_key)
-        key_t[...] = s_key[...].T
-        arrived(1, head, 0)
-        project(head, 0, s_query)
-        teacher_weights(cfg, lanes)
-
-        def one_block(step):
-            probability = probs_by_key(s_key[...], s_query[block_rows(step), :])
-            student_p[step] = probability
-            if student_w is not None:
-                student_w[step] = probability.astype(jnp.bfloat16)
-
-        run_blocks(one_block)
-        grad_key[...] = jnp.zeros_like(grad_key)
-        grad_value[...] = jnp.zeros_like(grad_value)
-        arrived(1, head, 2)
-        project(head, 2, s_value)
-        value_t[...] = s_value[...].T
-
-        def one_block(step):
-            attended = dot_f32(value_t[...], student_weights(step)).T
-            student[block_rows(step), lanes] = attended.astype(jnp.bfloat16)
-
-        run_blocks(one_block)
-        each_out(head, "start")
-        value_t[...] = heads[2, cfg, :, lanes].T
-
-        def one_block(step):
-            attended = dot_f32(value_t[...], teacher_w[step]).T.astype(jnp.bfloat16)
-            target[block_rows(step), :] = weighting(cfg) * attended.astype(jnp.float32)
-
-        run_blocks(one_block)
-        swap_copy(head).wait_recv()
-
-        def one_block(step):
-            rows = block_rows(step)
-            probability = student_p[step]
-            aim = target[rows, :] + weighted_in[head, rows, :].astype(jnp.float32)
-            error = student[rows, lanes].astype(jnp.float32) - aim
-            upstream = (error * out_scale).astype(jnp.bfloat16)
-            grad_value[...] += dot_f32(student_weights(step), upstream)
-            prob_grad = dot_nt(s_value[...], upstream)
-            center = jnp.sum(probability * prob_grad, axis=0, keepdims=True)
-            score_grad = (probability * (prob_grad - center)).astype(jnp.bfloat16)
-            grad_key[...] += dot_f32(score_grad, s_query[rows, :])
-            grad_query[rows, :] = (dot_f32(key_t[...], score_grad).T * FACTOR).astype(
-                jnp.bfloat16
-            )
-
-        run_blocks(one_block)
-
-        gradients = (
-            grad_query[...],
-            (grad_key[...] * FACTOR).astype(jnp.bfloat16),
-            grad_value[...].astype(jnp.bfloat16),
-        )
-        for member, gradient in enumerate(gradients):
-            piece = dot_nt(gradient, up_own[member, :, lanes])
-            if head > 0:
-                piece = piece + back_sum[:, head_columns(member)]
-            if head < heads_here - 1:
-                back_sum[:, head_columns(member)] = piece
-            else:
-                back[:, head_columns(member)] = piece.astype(jnp.bfloat16)
-                for far_step in far_order:
-                    for step in range(1, inner):
-                        near_copy(member, far_step, step).start()
-        for member, gradient in enumerate(gradients):
-            low_rank = ranks[:, :, :, head_columns(member)].reshape(length, ADAPTER_RANK)
-            piece = dot_tn(low_rank, gradient).astype(jnp.bfloat16)
-            up_parts[:, member, :, lanes] = piece.reshape(up_groups, -1, HDIM)
-
-    each_up("start")
-    own_store = pltpu.make_async_copy(
-        student.at[own_rows, :], tokens_ref.at[:, aligned(me, columns)], local_sem.at[6]
-    )
-
-    @pl.when(diagonal)
-    def _():
-        own_store.start()
-        up_in[0, 0, 0] = up_parts[cfg * dp_count + dp]
-
-    down_rows = hidden_t.shape[0] // outer
-
-    def gather_columns():
-        for step in range(1, groups):
-            cols_copy(step).wait_recv()
-        hidden_t[...] = hidden_all[...].reshape(groups * tok_here, -1).T
-
     def reduce_near(member):
         lanes = head_columns(member)
         for far_step in far_order:
@@ -649,6 +558,112 @@
                 far_copy(member, far_step).start()
         return total
 
+    def push_back(head, member, gradient):
+        lanes = head_columns(member)
+        piece = dot_nt(gradient, up_own[member, :, head_columns(head)])
+        if head > 0:
+            piece = piece + back_sum[:, lanes]
+        if head < heads_here - 1:
+            back_sum[:, lanes] = piece
+            return
+        back[:, lanes] = piece.astype(jnp.bfloat16)
+        for far_step in far_order:
+            for step in range(1, inner):
+                near_copy(member, far_step, step).start()
+
+    totals = {}
+    for head in range(heads_here):
+        lanes = head_columns(head)
+        arrived(1, head, 1)
+        project(head, 1, s_key)
+        key_t[...] = s_key[...].T
+        arrived(1, head, 0)
+        project(head, 0, s_query)
+        teacher_weights(cfg, lanes)
+
+        def one_block(step):
+            probability = probs_by_key(s_key[...], s_query[block_rows(step), :])
+            student_p[step] = probability
+            if student_w is not None:
+                student_w[step] = probability.astype(jnp.bfloat16)
+
+        run_blocks(one_block)
+        grad_key[...] = jnp.zeros_like(grad_key)
+        grad_value[...] = jnp.zeros_like(grad_value)
+        arrived(1, head, 2)
+        project(head, 2, s_value)
+        value_t[...] = s_value[...].T
+
+        def one_block(step):
+            attended = dot_f32(value_t[...], student_weights(step)).T
+            student[block_rows(step), lanes] = attended.astype(jnp.bfloat16)
+
+        run_blocks(one_block)
+        each_out(head, "start")
+        value_t[...] = heads[2, cfg, :, lanes].T
+
+        def one_block(step):
+            attended = dot_f32(value_t[...], teacher_w[step]).T.astype(jnp.bfloat16)
+            target[block_rows(step), :] = weighting(cfg) * attended.astype(jnp.float32)
+
+        run_blocks(one_block)
+        swap_copy(head).wait_recv()
+
+        def one_block(step):
+            rows = block_rows(step)
+            aim = target[rows, :] + weighted_in[head, rows, :].astype(jnp.float32)
+            error = student[rows, lanes].astype(jnp.float32) - aim
+            upstream[rows, :] = (error * out_scale).astype(jnp.bfloat16)
+            grad_value[...] += dot_f32(student_weights(step), upstream[rows, :])
+
+        run_blocks(one_block)
+        last = head == heads_here - 1
+        gradients = {2: grad_value[...].astype(jnp.bfloat16)}
+        push_back(head, 2, gradients[2])
+
+        def one_block(step):
+            rows = block_rows(step)
+            probability = student_p[step]
+            prob_grad = dot_nt(s_value[...], upstream[rows, :])
+            center = jnp.sum(probability * prob_grad, axis=0, keepdims=True)
+            score_grad = (probability * (prob_grad - center)).astype(jnp.bfloat16)
+            grad_key[...] += dot_f32(score_grad, s_query[rows, :])
+            grad_query[rows, :] = (dot_f32(key_t[...], score_grad).T * FACTOR).astype(
+                jnp.bfloat16
+            )
+
+        run_blocks(one_block)
+        if last:
+            totals[2] = reduce_near(2)
+        gradients[1] = (grad_key[...] * FACTOR).astype(jnp.bfloat16)
+        push_back(head, 1, gradients[1])
+        gradients[0] = grad_query[...]
+        push_back(head, 0, gradients[0])
+        if last:
+            totals[1] = reduce_near(1)
+            totals[0] = reduce_near(0)
+        for member, gradient in gradients.items():
+            low_rank = ranks[:, :, :, head_columns(member)].reshape(length, ADAPTER_RANK)
+            piece = dot_tn(low_rank, gradient).astype(jnp.bfloat16)
+            up_parts[:, member, :, lanes] = piece.reshape(up_groups, -1, HDIM)
+
+    each_up("start")
+    own_store = pltpu.make_async_copy(
+        student.at[own_rows, :], tokens_ref.at[:, aligned(me, columns)], local_sem.at[6]
+    )
+
+    @pl.when(diagonal)
+    def _():
+        own_store.start()
+        up_in[0, 0, 0] = up_parts[cfg * dp_count + dp]
+
+    down_rows = hidden_t.shape[0] // outer
+
+    def gather_columns():
+        for step in range(1, groups):
+            cols_copy(step).wait_recv()
+        hidden_t[...] = hidden_all[...].reshape(groups * tok_here, -1).T
+
     def reduce_far(member, total):
         lanes = head_columns(member)
         for step in range(1, outer):
@@ -680,18 +695,16 @@
         for step in range(1, outer):
             down_copy(member, step).start()
 
-    totals = {}
-    for turn in range(6):
-        if turn < 3:
-            totals[turn] = reduce_near(turn)
-        if 1 <= turn < 4:
-            reduce_far(turn - 1, totals[turn - 1])
-        if turn == 1:
-            gather_columns()
-        if 2 <= turn < 5:
-            spread(turn - 2)
-        if turn >= 3:
-            contract(turn - 3)
+    reduce_far(2, totals[2])
+    gather_columns()
+    reduce_far(1, totals[1])
+    spread(2)
+    contract(2)
+    reduce_far(0, totals[0])
+    spread(1)
+    contract(1)
+    spread(0)
+    contract(0)
 
     each_up("wait_recv")
     up_total = up_in[up_steps[0]].astype(jnp.float32)
@@ -699,7 +712,7 @@
         up_total = up_total + up_in[steps].astype(jnp.float32)
     grad_up_ref[...] = up_total
 
-    for member in range(3):
+    for member in (2, 1, 0):
         lanes = head_columns(member)
         down_total = down_out[far, :, lanes].astype(jnp.float32)
         for step in range(1, outer):
@@ -803,6 +816,7 @@
         bf16(length, HDIM),
         bf16(HDIM, length),
         bf16(HDIM, length),
+        bf16(length, HDIM),
         bf16(length, HDIM),
         f32(length, HDIM),
         f32(length, HDIM),

time: 120 us -> 120 us (level)
  no operation moved by 1% of the time
where the time goes in v5:
time: 120 us
  Pallas kernels  119 us (99%)
    pallas_call x1, Pallas kernels, run_step(): pl.pallas_call(with_gaps(functools.partial(step_kernel, sizes, 1.0 / math...  117 us

profile of v5, /device:TPU:0, one launch (start us, length us, event | category | flops | bytes accessed | tf_op | source)
XLA Modules:
  0.0 120.1 jit_solution(17746980049199689154)
XLA Ops:
  0.6 117.4 %step.1 = (bf16[128,2048]{1,0:T(8,128)(2,1)}, f32[3,96,128]{2,1,0:T(8,128)}, f32[3,32,256]{2,1,0:T(8,128)}) custom-call(s32[2]{0:T(128)} %bitcast.11, s32[2]{0:T(128)} %bitcast.12, bf16[2,128,2048]{2,1,0:T(8,128)(2,1)} %bitcast.7, bf16[2,128,2048]{2,1,0:T(8,128)(2,1)} %bitcast.8, bf16[2,128,2048]{2,1,0:T(8,128)(2,1)} %bitcast.9, bf16[128,3072]{1,0:T(8,128)(2,1)} %bitcast.10, ...), custom_call_target="tpu_custom_call" | custom-call | tf_op jit(solution)/shard_map/step/pallas_call | solution.py:854
  118.0 2.0 %emit.1 = (bf16[128,2048]{1,0:T(8,128)(2,1)}, f32[3,96,128]{2,1,0:T(8,128)}, f32[3,32,256]{2,1,0:T(8,128)}) custom-call(bf16[128,2048]{1,0:T(8,128)(2,1)} %get-tuple-element.9.refs_0_, f32[3,96,128]{2,1,0:T(8,128)} %get-tuple-element.10.refs_1_, f32[3,32,256]{2,1,0:T(8,128)} %get-tuple-element.11.refs_2_), custom_call_target="tpu_custom_call" | custom-call | tf_op jit(solution)/shard_map/emit/pallas_call | solution.py:893

commit v6 on v5

--- a/solution.py
+++ b/solution.py
@@ -219,14 +219,6 @@
         )
         for member in range(3)
     ]
-    for load in loads:
-        load.start()
-
-    @pl.when(diagonal)
-    def _():
-        for load in own_loads:
-            load.start()
-
     barrier = pltpu.get_barrier_semaphore()
     for step in range(1, count * inner):
         peer_near = lax.rem(near + step // inner % inner, inner)
@@ -413,6 +405,24 @@
             {"seq": peer * inner + near},
         )
 
+    def weighting(half):
+        scale = work_facts[1 + half]
+        return jnp.where(cfg == 0, scale, 1.0 - scale)
+
+    phases = [(phase, head) for phase in range(2) for head in range(heads_here)]
+    sends = [(phase, head, member) for phase, head in phases for member in (1, 0, 2)]
+    early_sends, late_sends = sends[:-3], sends[-3:]
+    loads[0].start()
+    loads[1].start()
+    pl.semaphore_wait(barrier, count * inner + groups - 2)
+    each_field(*sends[0], "start")
+    loads[2].start()
+
+    @pl.when(diagonal)
+    def _():
+        for load in own_loads:
+            load.start()
+
     def guide_scale(half):
         return 1.0 + 0.5 * guide_ref[half].astype(jnp.float32)
 
@@ -425,15 +435,6 @@
     facts[0] = modulation
     for half in range(2):
         facts[1 + half] = jnp.full((1, ADAPTER_RANK), guide_scale(half), jnp.float32)
-
-    def weighting(half):
-        scale = work_facts[1 + half]
-        return jnp.where(cfg == 0, scale, 1.0 - scale)
-
-    phases = [(phase, head) for phase in range(2) for head in range(heads_here)]
-    sends = [(phase, head, member) for phase, head in phases for member in (1, 0, 2)]
-    pl.semaphore_wait(barrier, count * inner + groups - 2)
-    each_field(*sends[0], "start")
 
     @pl.when(diagonal)
     def _():
@@ -590,6 +591,9 @@
         run_blocks(one_block)
         grad_key[...] = jnp.zeros_like(grad_key)
         grad_value[...] = jnp.zeros_like(grad_value)
+        if head == heads_here - 1:
+            for turn in early_sends:
+                each_field(*turn, "wait_send")
         arrived(1, head, 2)
         project(head, 2, s_value)
         value_t[...] = s_value[...].T
@@ -695,12 +699,38 @@
         for step in range(1, outer):
             down_copy(member, step).start()
 
+    for turn in late_sends:
+        each_field(*turn, "wait_send")
+    for head in range(heads_here):
+        swap_copy(head).wait_send()
+
+        @pl.when(cfg == 0)
+        def _():
+            for member in range(3):
+                pass_copy(head, member).wait_send()
+
+        if head < heads_here - 1:
+            each_out(head, "wait")
+    for hop in range(outer - 1):
+        rank_step(hop, "wait_send", ranks_leave)
+    for step in range(inner):
+        when_remote((step,), fan_copy(step).wait_send)
+
     reduce_far(2, totals[2])
     gather_columns()
+    for step in range(1, groups):
+        cols_copy(step).wait_send()
+    for member in range(3):
+        for far_step in range(outer):
+            for step in range(1, inner):
+                near_copy(member, far_step, step).wait_send()
     reduce_far(1, totals[1])
     spread(2)
     contract(2)
     reduce_far(0, totals[0])
+    for member in range(3):
+        for step in range(1, outer):
+            far_copy(member, step).wait_send()
     spread(1)
     contract(1)
     spread(0)
@@ -726,23 +756,7 @@
         for step in range(1, inner):
             facts_copy(step).wait_send()
 
-    for turn in sends:
-        each_field(*turn, "wait_send")
-    for head in range(heads_here):
-        swap_copy(head).wait_send()
-
-        @pl.when(cfg == 0)
-        def _():
-            for member in range(3):
-                pass_copy(head, member).wait_send()
-
-        each_out(head, "wait")
-    for hop in range(outer - 1):
-        rank_step(hop, "wait_send", ranks_leave)
-    for step in range(inner):
-        when_remote((step,), fan_copy(step).wait_send)
-    for step in range(1, groups):
-        cols_copy(step).wait_send()
+    each_out(heads_here - 1, "wait")
     each_up("wait_send")
     for member in range(3):
         for pair_step in range(pairs):
@@ -750,12 +764,8 @@
                 low_copy(member, pair_step).wait_send()
             for step in range(1, dp_count):
                 share_copy(member, pair_step, step).wait_send()
-        for far_step in range(outer):
-            if far_step > 0:
-                far_copy(member, far_step).wait_send()
-                down_copy(member, far_step).wait_send()
-            for step in range(1, inner):
-                near_copy(member, far_step, step).wait_send()
+        for step in range(1, outer):
+            down_copy(member, step).wait_send()
 
 
 def with_gaps(kernel, scratch, skipped):

time: 120 us -> 120 us (level)
  no operation moved by 1% of the time
where the time goes in v6:
time: 120 us
  Pallas kernels  119 us (99%)
    pallas_call x1, Pallas kernels, run_step(): pl.pallas_call(with_gaps(functools.partial(step_kernel, sizes, 1.0 / math...  117 us

profile of v6, /device:TPU:0, one launch (start us, length us, event | category | flops | bytes accessed | tf_op | source)
XLA Modules:
  0.0 120.0 jit_solution(6950282188380357316)
XLA Ops:
  0.6 117.2 %step.1 = (bf16[128,2048]{1,0:T(8,128)(2,1)}, f32[3,96,128]{2,1,0:T(8,128)}, f32[3,32,256]{2,1,0:T(8,128)}) custom-call(s32[2]{0:T(128)} %bitcast.11, s32[2]{0:T(128)} %bitcast.12, bf16[2,128,2048]{2,1,0:T(8,128)(2,1)} %bitcast.7, bf16[2,128,2048]{2,1,0:T(8,128)(2,1)} %bitcast.8, bf16[2,128,2048]{2,1,0:T(8,128)(2,1)} %bitcast.9, bf16[128,3072]{1,0:T(8,128)(2,1)} %bitcast.10, ...), custom_call_target="tpu_custom_call" | custom-call | tf_op jit(solution)/shard_map/step/pallas_call | solution.py:864
  117.9 2.0 %emit.1 = (bf16[128,2048]{1,0:T(8,128)(2,1)}, f32[3,96,128]{2,1,0:T(8,128)}, f32[3,32,256]{2,1,0:T(8,128)}) custom-call(bf16[128,2048]{1,0:T(8,128)(2,1)} %get-tuple-element.9.refs_0_, f32[3,96,128]{2,1,0:T(8,128)} %get-tuple-element.10.refs_1_, f32[3,32,256]{2,1,0:T(8,128)} %get-tuple-element.11.refs_2_), custom_call_target="tpu_custom_call" | custom-call | tf_op jit(solution)/shard_map/emit/pallas_call | solution.py:903

commit v7 on v6

--- a/solution.py
+++ b/solution.py
@@ -164,7 +164,8 @@
     group = dp * pairs + pair
     work_block = far * inner + part
     own_rows = aligned(me, tok_here)
-    grid_steps = [(far_step, near_step) for far_step in range(outer) for near_step in range(inner)]
+    far_order = sorted(range(outer), key=lambda step: (step == 0, abs(2 * step - outer)))
+    grid_steps = [(far_step, near_step) for far_step in far_order for near_step in range(inner)]
     up_steps = [
         (cfg_step, bundle_step, near_step)
         for cfg_step in range(2)
@@ -483,7 +484,6 @@
         for load in own_loads:
             load.wait()
 
-    far_order = sorted(range(outer), key=lambda step: (step == 0, abs(2 * step - outer)))
 
     def run_blocks(one_block):
         unroll = 2 if blocks % 2 == 0 else 1
@@ -651,7 +651,6 @@
             piece = dot_tn(low_rank, gradient).astype(jnp.bfloat16)
             up_parts[:, member, :, lanes] = piece.reshape(up_groups, -1, HDIM)
 
-    each_up("start")
     own_store = pltpu.make_async_copy(
         student.at[own_rows, :], tokens_ref.at[:, aligned(me, columns)], local_sem.at[6]
     )
@@ -725,6 +724,7 @@
             for step in range(1, inner):
                 near_copy(member, far_step, step).wait_send()
     reduce_far(1, totals[1])
+    each_up("start")
     spread(2)
     contract(2)
     reduce_far(0, totals[0])

time: 120 us -> 120 us (level)
  no operation moved by 1% of the time
where the time goes in v7:
time: 120 us
  Pallas kernels  119 us (99%)
    pallas_call x1, Pallas kernels, run_step(): pl.pallas_call(with_gaps(functools.partial(step_kernel, sizes, 1.0 / math...  117 us

profile of v7, /device:TPU:0, one launch (start us, length us, event | category | flops | bytes accessed | tf_op | source)
XLA Modules:
  0.0 119.6 jit_solution(16456903064084266148)
XLA Ops:
  0.6 116.9 %step.1 = (bf16[128,2048]{1,0:T(8,128)(2,1)}, f32[3,96,128]{2,1,0:T(8,128)}, f32[3,32,256]{2,1,0:T(8,128)}) custom-call(s32[2]{0:T(128)} %bitcast.11, s32[2]{0:T(128)} %bitcast.12, bf16[2,128,2048]{2,1,0:T(8,128)(2,1)} %bitcast.7, bf16[2,128,2048]{2,1,0:T(8,128)(2,1)} %bitcast.8, bf16[2,128,2048]{2,1,0:T(8,128)(2,1)} %bitcast.9, bf16[128,3072]{1,0:T(8,128)(2,1)} %bitcast.10, ...), custom_call_target="tpu_custom_call" | custom-call | tf_op jit(solution)/shard_map/step/pallas_call | solution.py:864
  117.5 2.0 %emit.1 = (bf16[128,2048]{1,0:T(8,128)(2,1)}, f32[3,96,128]{2,1,0:T(8,128)}, f32[3,32,256]{2,1,0:T(8,128)}) custom-call(bf16[128,2048]{1,0:T(8,128)(2,1)} %get-tuple-element.9.refs_0_, f32[3,96,128]{2,1,0:T(8,128)} %get-tuple-element.10.refs_1_, f32[3,32,256]{2,1,0:T(8,128)} %get-tuple-element.11.refs_2_), custom_call_target="tpu_custom_call" | custom-call | tf_op jit(solution)/shard_map/emit/pallas_call | solution.py:903
